TPU v7x, 16 devices: a whole 2x2x2 slice. The times are simulated.
16 devices in a mesh: dp: 2 (over z), sp: 8 (over y, x, core).
Axes of the slice: x: 2, y: 2, z: 2, core: 2. Of those that a mesh axis runs over, the one named last changes fastest.
Arguments:
- images: float32 [12, 256, 256, 3], P('dp', 'sp'), parts along dimension 0
- w_patch: bfloat16 [16, 16, 3, 1024], replicated
- b_patch: float32 [1024], replicated
- pos_embed: bfloat16 [256, 1024], P('sp')
- ln1_gain: float32 [1024], replicated
- ln1_bias: float32 [1024], replicated
- w_qkv: bfloat16 [1024, 3, 16, 64], replicated
- b_qkv: float32 [3, 16, 64], replicated
- w_out: bfloat16 [16, 64, 1024], replicated
- b_out: float32 [1024], replicated
- ln2_gain: float32 [1024], replicated
- ln2_bias: float32 [1024], replicated
- w_fc1: bfloat16 [1024, 4096], replicated
- b_fc1: float32 [4096], replicated
- w_fc2: bfloat16 [4096, 1024], replicated
- b_fc2: float32 [1024], replicated
Outputs:
- output: bfloat16 [12, 256, 1024], P('dp', 'sp'), parts along dimension 0
There are 2 independent parts. A program takes and returns all parts, laid end to end along the dimension named above; an argument that names none is the same for every part.
All inputs are finite; a program needn't handle non-finite values.
Results may differ from a plain program's by a relative error of at most 0.0125094.
Values are sent between devices in bfloat16 or wider.
A program may use at most 1 GiB of HBM per device.

v0:
```python
import math
import jax
import jax.numpy as jnp
from jax import lax
from jax.sharding import PartitionSpec as P

LN_EPS = 1e-6


def layer_norm(x_in, ln_gain, ln_bias):
    row_mean = jnp.mean(x_in, axis=-1, keepdims=True)
    centered = x_in - row_mean
    variance = jnp.mean(centered * centered, axis=-1, keepdims=True)
    return centered * lax.rsqrt(variance + LN_EPS) * ln_gain + ln_bias


def embed_tokens(images, w_patch, b_patch, pos_embed):
    num_images, num_rows, num_cols, channels = images.shape
    patch_len = w_patch.shape[0]
    grid_rows = num_rows // patch_len
    grid_cols = num_cols // patch_len
    pixels = images.astype(jnp.bfloat16).reshape(num_images, grid_rows, patch_len, grid_cols, patch_len, channels)
    patch_embed = jnp.einsum('bypxqc,pqcd->byxd', pixels, w_patch, preferred_element_type=jnp.float32)
    patch_embed = patch_embed.reshape(num_images, grid_rows * grid_cols, w_patch.shape[3])
    return (patch_embed + b_patch + pos_embed.astype(jnp.float32)).astype(jnp.bfloat16)


def attend(queries, keys_all, values_all):
    num_images, n_query, num_heads, head_dim = queries.shape
    tile_len = math.gcd(n_query, 128)
    score_scale = head_dim ** -0.5

    def one_image(operands):
        q_img, k_img, v_img = operands

        def one_group(q_group):
            scores = jnp.einsum('qhe,khe->hqk', q_group, k_img, preferred_element_type=jnp.float32) * score_scale
            att_weights = jax.nn.softmax(scores, axis=-1).astype(jnp.bfloat16)
            return jnp.einsum('hqk,khe->qhe', att_weights, v_img, preferred_element_type=jnp.float32).astype(jnp.bfloat16)

        grouped = lax.map(one_group, q_img.reshape(n_query // tile_len, tile_len, num_heads, head_dim))
        return grouped.reshape(n_query, num_heads, head_dim)

    return lax.map(one_image, (queries, keys_all, values_all))


def finish_layer(x_zero, attended, w_out, b_out, ln2_gain, ln2_bias, w_fc1, b_fc1, w_fc2, b_fc2):
    residual = x_zero.astype(jnp.float32) + jnp.einsum('bnhe,hed->bnd', attended, w_out, preferred_element_type=jnp.float32) + b_out
    normed_two = layer_norm(residual, ln2_gain, ln2_bias).astype(jnp.bfloat16)
    hidden = jax.nn.gelu(jnp.einsum('bnd,df->bnf', normed_two, w_fc1, preferred_element_type=jnp.float32) + b_fc1, approximate=True).astype(jnp.bfloat16)
    return (residual + jnp.einsum('bnf,fd->bnd', hidden, w_fc2, preferred_element_type=jnp.float32) + b_fc2).astype(jnp.bfloat16)


def solution(mesh):
    def device_step(images, w_patch, b_patch, pos_embed, ln1_gain, ln1_bias, w_qkv, b_qkv, w_out, b_out, ln2_gain, ln2_bias, w_fc1, b_fc1, w_fc2, b_fc2):
        x_zero = embed_tokens(images, w_patch, b_patch, pos_embed)
        normed = layer_norm(x_zero.astype(jnp.float32), ln1_gain, ln1_bias).astype(jnp.bfloat16)
        qkv_proj = (jnp.einsum('bnd,dthe->bnthe', normed, w_qkv, preferred_element_type=jnp.float32) + b_qkv).astype(jnp.bfloat16)
        key_value = lax.all_gather(qkv_proj[:, :, 1:], 'sp', axis=1, tiled=True)
        attended = attend(qkv_proj[:, :, 0], key_value[:, :, 0], key_value[:, :, 1])
        return finish_layer(x_zero, attended, w_out, b_out, ln2_gain, ln2_bias, w_fc1, b_fc1, w_fc2, b_fc2)

    in_specs = (P('dp', 'sp', None, None), P(), P(), P('sp', None), P(), P(), P(), P(), P(), P(), P(), P(), P(), P(), P(), P())
    return jax.shard_map(device_step, mesh=mesh, in_specs=in_specs, out_specs=P('dp', 'sp', None), check_vma=False)
```

profile of v0, /device:TPU:0, one launch (start us, length us, event | category | flops | bytes accessed | tf_op | source)
XLA Modules:
  0.0 181.5 jit_solution(16717505180819145918)
XLA Ops:
  8.7 2.7 %reshape.43 = bf16[6,2,16,16,16,3]{4,3,2,1,5,0:T(8,128)(2,1)} reshape(bf16[6,32,256,3]{2,1,3,0:T(8,128)(2,1)S(1)} %convert_element_type.39) | data formatting | bytes 589824 | tf_op jit(solution)/shard_map/reshape | solution.py:22
  11.3 6.4 %copy.26 = bf16[6,2,16,3,16,16]{2,1,5,4,0,3:T(2,128)(2,1)} copy(bf16[6,2,16,3,16,16]{5,2,4,1,3,0:T(8,128)(2,1)} %bitcast.126) | data formatting | bytes 589824 | tf_op jit(solution)/shard_map/bypxqc,pqcd->byxd/dot_general | solution.py:23
  17.7 4.3 %reshape.52 = bf16[6,32,3,16,16]{1,4,3,0,2:T(8,128)(2,1)S(1)} reshape(bf16[6,2,16,3,16,16]{2,1,5,4,0,3:T(2,128)(2,1)} %copy.26) | data formatting | bytes 589824 | tf_op jit(solution)/shard_map/bypxqc,pqcd->byxd/dot_general | solution.py:23
  22.1 2.0 %fusion.124 = (f32[6,32]{1,0:T(8,128)S(1)}, f32[6,32,1024]{2,1,0:T(8,128)S(1)}) fusion(f32[32,1024]{1,0:T(8,128)S(1)} %convert_element_type.40, f32[1024]{0:T(1024)S(1)} %copy-done.5, bf16[6,32,3,16,16]{1,4,3,0,2:T(8,128)(2,1)S(1)} %reshape.52, bf16[16,16,3,1024]{3,1,2,0:T(8,128)(2,1)} %param.19), kind=kOutput, calls=%fused_computation.79 | convolution fusion | flops 302972736 | bytes 2790144 | tf_op jit(solution)/shard_map/bypxqc,pqcd->byxd/dot_general | solution.py:23
  24.4 9.3 %add_convert_fusion = bf16[6,32,3,16,64]{4,1,3,2,0:T(8,128)(2,1)S(1)} fusion(f32[3,16,64]{2,1,0:T(8,128)S(1)} %copy-done.6, bf16[1024,3,16,64]{0,3,2,1:T(8,128)(2,1)} %param.24, f32[6,32,1024]{2,1,0:T(8,128)S(1)} %get-tuple-element.66, f32[1024]{0:T(1024)S(1)} %copy-done.8, f32[1024]{0:T(1024)S(1)} %copy-done.9, f32[6,32]{1,0:T(8,128)S(1)} %add_rsqrt_fusion.1, ...), kind=kOutput, calls=%fused_computation.32 | convolution fusion | flops 1210122240 | bytes 8279552 | tf_op jit(solution)/shard_map/bnd,dthe->bnthe/dot_general | solution.py:58
  36.6 2.1 %slice_bitcast_fusion.2 = bf16[6,32,16,64]{3,1,2,0:T(8,128)(2,1)} fusion(bf16[6,32,3,16,64]{4,1,3,2,0:T(8,128)(2,1)} %copy-done.3), kind=kLoop, calls=%fused_computation.56 | loop fusion | bytes 786432 | tf_op jit(solution)/shard_map/squeeze | solution.py:60
  38.7 71.4 %all-gather.2.cloned.1.call-done = bf16[6,256,2,16,64]{4,1,3,2,0:T(8,128)(2,1)} async-done(((bf16[6,32,2,16,64]{4,1,3,2,0:T(8,128)(2,1)}), bf16[6,256,2,16,64]{4,1,3,2,0:T(8,128)(2,1)}) %all-gather.2.cloned.1.call-update) | async-done | bytes 6291472 | tf_op jit(solution)/shard_map/all_gather | solution.py:59
  110.1 10.6 %slice_bitcast_fusion = (bf16[6,256,16,64]{3,1,2,0:T(8,128)(2,1)}, bf16[6,256,16,64]{3,1,2,0:T(8,128)(2,1)}) fusion(bf16[6,256,2,16,64]{4,1,3,2,0:T(8,128)(2,1)} %all-gather.2.cloned.1.call-done), kind=kLoop, calls=%fused_computation.26 | loop fusion | bytes 12582912 | tf_op jit(solution)/shard_map/squeeze | solution.py:60
  120.7 6.7 %copy.20 = bf16[6,256,16,64]{1,3,2,0:T(8,128)(2,1)} copy(bf16[6,256,16,64]{3,1,2,0:T(8,128)(2,1)} %get-tuple-element.63) | data formatting | bytes 6291456 | tf_op jit(solution)/shard_map/while | solution.py:44
  127.4 6.7 %copy.19 = bf16[6,256,16,64]{1,3,2,0:T(8,128)(2,1)} copy(bf16[6,256,16,64]{3,1,2,0:T(8,128)(2,1)} %get-tuple-element.64) | data formatting | bytes 6291456 | tf_op jit(solution)/shard_map/while | solution.py:44
  134.1 26.5 %while.10 = (s32[]{:T(128)}, bf16[6,32,16,64]{3,1,2,0:T(8,128)(2,1)}, bf16[6,256,16,64]{1,3,2,0:T(8,128)(2,1)}, bf16[6,32,16,64]{3,1,2,0:T(8,128)(2,1)}, bf16[6,256,16,64]{1,3,2,0:T(8,128)(2,1)}, /*index=5*/s32[]{:T(128)}) while((s32[]{:T(128)}, bf16[6,32,16,64]{3,1,2,0:T(8,128)(2,1)}, bf16[6,256,16,64]{1,3,2,0:T(8,128)(2,1)}, ...), condition=%wide.region_5.6_spmd, body=%wide.region_2.5_spmd.sunk | while | flops 51282944 | bytes 1973325 | solution.py:44
  134.1 1.6 fusion.141
  135.7 2.9 %fusion.142 = bf16[6,32,16,64]{3,1,2,0:T(8,128)(2,1)} fusion(bf16[6,32,16,64]{3,1,2,0:T(8,128)(2,1)} %get-tuple-element.107, s32[]{:T(128)S(6)} %copy.47, bf16[6,256,16,64]{1,3,2,0:T(8,128)(2,1)} %get-tuple-element.114, f32[16,32]{1,0:T(8,128)S(1)} %fusion.141, bf16[6,256,16,64]{1,3,2,0:T(8,128)(2,1)} %get-tuple-element.116, ...), kind=kOutput, calls=%fused_computation.6.clone.1 | convolution fusion | flops 34112256 | bytes 1314816 | tf_op jit(solution)/shard_map/while/body/eval_jaxpr/while/body/eval_jaxpr/hqk,khe->qhe/dot_general | solution.py:39
  138.6 1.5 fusion.141
  140.1 2.9 %fusion.142 = bf16[6,32,16,64]{3,1,2,0:T(8,128)(2,1)} fusion(bf16[6,32,16,64]{3,1,2,0:T(8,128)(2,1)} %get-tuple-element.107, s32[]{:T(128)S(6)} %copy.47, bf16[6,256,16,64]{1,3,2,0:T(8,128)(2,1)} %get-tuple-element.114, f32[16,32]{1,0:T(8,128)S(1)} %fusion.141, bf16[6,256,16,64]{1,3,2,0:T(8,128)(2,1)} %get-tuple-element.116, ...), kind=kOutput, calls=%fused_computation.6.clone.1 | convolution fusion | flops 34112256 | bytes 1314816 | tf_op jit(solution)/shard_map/while/body/eval_jaxpr/while/body/eval_jaxpr/hqk,khe->qhe/dot_general | solution.py:39
  143.0 1.5 fusion.141
  144.5 2.9 %fusion.142 = bf16[6,32,16,64]{3,1,2,0:T(8,128)(2,1)} fusion(bf16[6,32,16,64]{3,1,2,0:T(8,128)(2,1)} %get-tuple-element.107, s32[]{:T(128)S(6)} %copy.47, bf16[6,256,16,64]{1,3,2,0:T(8,128)(2,1)} %get-tuple-element.114, f32[16,32]{1,0:T(8,128)S(1)} %fusion.141, bf16[6,256,16,64]{1,3,2,0:T(8,128)(2,1)} %get-tuple-element.116, ...), kind=kOutput, calls=%fused_computation.6.clone.1 | convolution fusion | flops 34112256 | bytes 1314816 | tf_op jit(solution)/shard_map/while/body/eval_jaxpr/while/body/eval_jaxpr/hqk,khe->qhe/dot_general | solution.py:39
  148.9 2.9 %fusion.142 = bf16[6,32,16,64]{3,1,2,0:T(8,128)(2,1)} fusion(bf16[6,32,16,64]{3,1,2,0:T(8,128)(2,1)} %get-tuple-element.107, s32[]{:T(128)S(6)} %copy.47, bf16[6,256,16,64]{1,3,2,0:T(8,128)(2,1)} %get-tuple-element.114, f32[16,32]{1,0:T(8,128)S(1)} %fusion.141, bf16[6,256,16,64]{1,3,2,0:T(8,128)(2,1)} %get-tuple-element.116, ...), kind=kOutput, calls=%fused_computation.6.clone.1 | convolution fusion | flops 34112256 | bytes 1314816 | tf_op jit(solution)/shard_map/while/body/eval_jaxpr/while/body/eval_jaxpr/hqk,khe->qhe/dot_general | solution.py:39
  151.8 1.5 fusion.141
  153.3 2.9 %fusion.142 = bf16[6,32,16,64]{3,1,2,0:T(8,128)(2,1)} fusion(bf16[6,32,16,64]{3,1,2,0:T(8,128)(2,1)} %get-tuple-element.107, s32[]{:T(128)S(6)} %copy.47, bf16[6,256,16,64]{1,3,2,0:T(8,128)(2,1)} %get-tuple-element.114, f32[16,32]{1,0:T(8,128)S(1)} %fusion.141, bf16[6,256,16,64]{1,3,2,0:T(8,128)(2,1)} %get-tuple-element.116, ...), kind=kOutput, calls=%fused_computation.6.clone.1 | convolution fusion | flops 34112256 | bytes 1314816 | tf_op jit(solution)/shard_map/while/body/eval_jaxpr/while/body/eval_jaxpr/hqk,khe->qhe/dot_general | solution.py:39
  156.2 1.5 fusion.141
  157.7 2.9 %fusion.142 = bf16[6,32,16,64]{3,1,2,0:T(8,128)(2,1)} fusion(bf16[6,32,16,64]{3,1,2,0:T(8,128)(2,1)} %get-tuple-element.107, s32[]{:T(128)S(6)} %copy.47, bf16[6,256,16,64]{1,3,2,0:T(8,128)(2,1)} %get-tuple-element.114, f32[16,32]{1,0:T(8,128)S(1)} %fusion.141, bf16[6,256,16,64]{1,3,2,0:T(8,128)(2,1)} %get-tuple-element.116, ...), kind=kOutput, calls=%fused_computation.6.clone.1 | convolution fusion | flops 34112256 | bytes 1314816 | tf_op jit(solution)/shard_map/while/body/eval_jaxpr/while/body/eval_jaxpr/hqk,khe->qhe/dot_general | solution.py:39
  160.7 1.9 %fusion.125 = (f32[6,32]{1,0:T(8,128)S(1)}, f32[6,32,1024]{2,1,0:T(8,128)S(1)}) fusion(f32[1024]{0:T(1024)S(1)} %copy-done.10, f32[6,32,1024]{2,1,0:T(8,128)S(1)} %copy-done.2, bf16[6,32,16,64]{3,1,2,0:T(8,128)(2,1)} %get-tuple-element.47, bf16[16,64,1024]{2,1,0:T(8,128)(2,1)S(1)} %copy-done), kind=kOutput, calls=%fused_computation.80 | convolution fusion | flops 403242816 | bytes 4068096 | tf_op jit(solution)/shard_map/bnhe,hed->bnd/dot_general | solution.py:48
  163.7 10.9 %fusion.96 = bf16[6,32,1024]{2,1,0:T(8,128)(2,1)} fusion(f32[6,32,1024]{2,1,0:T(8,128)} %copy-done.4, bf16[4096,1024]{1,0:T(8,128)(2,1)} %param.32, bf16[1024,4096]{1,0:T(8,128)(2,1)} %param.30, f32[4096]{0:T(1024)S(1)} %copy-done.7, f32[1024]{0:T(1024)S(1)} %copy-done.11, f32[1024]{0:T(1024)S(1)} %copy-done.12, f32[1024]{0:T(1024)S(1)} %copy-done.13, ...), kind=kOutput, calls=%fused_computation.55 | convolution fusion | flops 3230662656 | bytes 17987072 | tf_op jit(solution)/shard_map/bnf,fd->bnd/dot_general | solution.py:51
  (41 shorter events, 7.9 us)
Async XLA Ops:
  6.5 154.1 %copy-start = (bf16[16,64,1024]{2,1,0:T(8,128)(2,1)S(1)}, bf16[16,64,1024]{2,1,0:T(8,128)(2,1)}, u32[]{:S(2)}) copy-start(bf16[16,64,1024]{2,1,0:T(8,128)(2,1)} %param.26) | copy-start | bytes 6291460
  6.5 103.6 %all-gather.2.cloned.1.call-start = ((), (), s32[]{:S(2)}) async-start(), calls=%async_computation | async-start | bytes 14155776 | tf_op jit(solution)/shard_map/all_gather | solution.py:59
  11.3 10.7 %copy-start.5 = (f32[1024]{0:T(1024)S(1)}, f32[1024]{0:T(1024)}, u32[]{:S(2)}) copy-start(f32[1024]{0:T(1024)} %param.20) | copy-start | bytes 12292
  17.7 6.6 %copy-start.6 = (f32[3,16,64]{2,1,0:T(8,128)S(1)}, f32[3,16,64]{2,1,0:T(8,128)}, u32[]{:S(2)}) copy-start(f32[3,16,64]{2,1,0:T(8,128)} %param.25) | copy-start | bytes 36868
  17.7 6.6 %copy-start.8 = (f32[1024]{0:T(1024)S(1)}, f32[1024]{0:T(1024)}, u32[]{:S(2)}) copy-start(f32[1024]{0:T(1024)} %param.23) | copy-start | bytes 12292
  17.7 6.6 %copy-start.9 = (f32[1024]{0:T(1024)S(1)}, f32[1024]{0:T(1024)}, u32[]{:S(2)}) copy-start(f32[1024]{0:T(1024)} %param.22) | copy-start | bytes 12292
  24.1 9.6 %copy-start.1 = (f32[6,32,1024]{2,1,0:T(8,128)}, f32[6,32,1024]{2,1,0:T(8,128)S(1)}, u32[]{:S(2)}) copy-start(f32[6,32,1024]{2,1,0:T(8,128)S(1)} %get-tuple-element.66) | copy-start | bytes 2359300
  33.7 1.4 copy-start.3
  134.1 26.5 %copy-start.2 = (f32[6,32,1024]{2,1,0:T(8,128)S(1)}, f32[6,32,1024]{2,1,0:T(8,128)}, u32[]{:S(2)}) copy-start(f32[6,32,1024]{2,1,0:T(8,128)} %copy-done.1) | copy-start | bytes 2359300
  134.1 26.5 %copy-start.10 = (f32[1024]{0:T(1024)S(1)}, f32[1024]{0:T(1024)}, u32[]{:S(2)}) copy-start(f32[1024]{0:T(1024)} %param.27) | copy-start | bytes 12292
  160.7 3.0 %copy-start.7 = (f32[4096]{0:T(1024)S(1)}, f32[4096]{0:T(1024)}, u32[]{:S(2)}) copy-start(f32[4096]{0:T(1024)} %param.31) | copy-start | bytes 49156
  160.7 3.0 %copy-start.11 = (f32[1024]{0:T(1024)S(1)}, f32[1024]{0:T(1024)}, u32[]{:S(2)}) copy-start(f32[1024]{0:T(1024)} %param.33) | copy-start | bytes 12292
  160.7 3.0 %copy-start.12 = (f32[1024]{0:T(1024)S(1)}, f32[1024]{0:T(1024)}, u32[]{:S(2)}) copy-start(f32[1024]{0:T(1024)} %param.29) | copy-start | bytes 12292
  160.7 3.0 %copy-start.13 = (f32[1024]{0:T(1024)S(1)}, f32[1024]{0:T(1024)}, u32[]{:S(2)}) copy-start(f32[1024]{0:T(1024)} %param.28) | copy-start | bytes 12292
  162.6 0.9 copy-start.4
Sparse Core Ops, SparseCore 0:
  36.7 73.3 all-gather.1
where the time goes:
time: 182 us; the launch traced here: 181 us
  waiting for transfers between devices  71.4 us (39%)
  matrix products  50.6 us (28%)
  local copies, waits for them, and re-layouts  43.3 us (24%)
  between operations  13.6 us (7%)
  other arithmetic  2.55 us (1%)
    all_gather x1, waiting for transfers between devices, device_step(): key_value = lax.all_gather(qkv_proj[:, :, 1:], 'sp', axis=1, tiled=True)  71.4 us
    dot_general x6, matrix products, one_group(): jnp.einsum('hqk,khe->qhe', att_weights, v_img, preferred_element_type=jnp...  17.5 us
    while x2, local copies, waits for them, and re-layouts, attend(): return lax.map(one_image, (queries, keys_all, values_all))  13.4 us
    squeeze x2, local copies, waits for them, and re-layouts, device_step(): attended = attend(qkv_proj[:, :, 0], key_value[:, :, 0], key_value[:, :, 1])  12.7 us
    dot_general x1, matrix products, finish_layer(): jnp.einsum('bnf,fd->bnd', hidden, w_fc2, preferred_element_type=jnp.float32)  10.9 us
    dot_general x2, local copies, waits for them, and re-layouts, embed_tokens(): jnp.einsum('bypxqc,pqcd->byxd', pixels, w_patch, preferred_element_type=j...  10.7 us
    dot_general x1, matrix products, device_step(): jnp.einsum('bnd,dthe->bnthe', normed, w_qkv, preferred_element_type=jnp.f...  9.28 us
    sub x6, matrix products, one_group(): att_weights = jax.nn.softmax(scores, axis=-1).astype(jnp.bfloat16)  9.05 us
  transfers between devices with their start and end apart: 1, of which 1 were waited for; matrix products, arithmetic and copies ran while one was open for 1% of the time, Pallas kernels for 0%

commit v1 on v0

v1 whole, which is shorter than its diff:
```python
import functools
import math
import jax
import jax.numpy as jnp
from jax import lax
from jax.experimental import pallas as pl
from jax.experimental.pallas import tpu as pltpu
from jax.sharding import PartitionSpec as P

LN_EPS = 1e-6
F32 = jnp.float32
BF16 = jnp.bfloat16
D = 1024
FF = 4096
IMAGES = 6
BLOCK = 32
TOKENS = 256
OWN = 192
N_FC1, W_FC1 = 8, 512
N_FC2, W_FC2 = 4, 256
EXP_SCALE = math.log2(math.e) / 8.0
MESH = pl.DeviceIdType.MESH
NT = (((1,), (1,)), ((), ()))


def as_row(vec):
    return jnp.concatenate([vec[i:i + 1, :] for i in range(vec.shape[0])], axis=1)


def norm_rows(x_in, gain, bias):
    centered = x_in - jnp.mean(x_in, axis=-1, keepdims=True)
    variance = jnp.mean(centered * centered, axis=-1, keepdims=True)
    return centered * lax.rsqrt(variance + LN_EPS) * gain + bias


def layer_kernel(
        img_hbm, wp_hbm, bp_hbm, pos_hbm, g1_hbm, c1_hbm, wqkv_hbm, bqkv_hbm, wo_hbm, bo_hbm, g2_hbm, c2_hbm,
        w1_hbm, b1_hbm, w2_hbm, b2_hbm,
        out_hbm,
        img, wp, pos, vecs, b1, bqkv, wqkv, wo, w1, w2,
        lhs, sel, pix, xs, xg, y1, qh, kh, vh, og, op, res, y2, hid, outs, b1row,
        in_sem, wqkv_sem, wo_sem, w1_sem, w2_sem,
        xsend, xrecv, fsend, frecv, osend, orecv, rsend, rrecv):
    dp = lax.axis_index("dp")
    me = lax.axis_index("sp")
    chip = me // 2
    core = me % 2
    mate = chip * 2 + (1 - core)
    cx = chip % 2
    cy = chip // 2

    def remote(src, dst, ssem, rsem, dev):
        return pltpu.make_async_remote_copy(
            src_ref=src, dst_ref=dst, send_sem=ssem, recv_sem=rsem, device_id=(dp, dev), device_id_type=MESH)

    def chip_at(k):
        return ((cy + k // 2) % 2) * 2 + (cx + k % 2) % 2

    barrier = pltpu.get_barrier_semaphore()
    for k in range(1, 8):
        pl.semaphore_signal(barrier, inc=1, device_id=(dp, (me + k) % 8), device_id_type=MESH)

    small = [(img_hbm, img), (wp_hbm, wp), (pos_hbm, pos)]
    for i, v in enumerate((bp_hbm, g1_hbm, c1_hbm, bo_hbm, g2_hbm, c2_hbm, b2_hbm)):
        small.append((v, vecs.at[i]))
    small.append((b1_hbm, b1))
    small_copies = [pltpu.make_async_copy(s, d, in_sem.at[i]) for i, (s, d) in enumerate(small)]
    for c in small_copies:
        c.start()
    bq_copy = pltpu.make_async_copy(bqkv_hbm.at[:, pl.ds(pl.multiple_of(core * 8, 8), 8), :], bqkv, in_sem.at[len(small)])
    bq_copy.start()
    wq_copies = [
        pltpu.make_async_copy(wqkv_hbm.at[pl.ds(pl.multiple_of(t * D + core * 512, 512), 512), :], wqkv.at[t], wqkv_sem.at[t])
        for t in range(3)]
    wo_copies = [
        pltpu.make_async_copy(wo_hbm.at[pl.ds(pl.multiple_of(((core + i) % 2) * 512, 512), 512), :], wo.at[i], wo_sem.at[i])
        for i in range(2)]
    w1_copies = [pltpu.make_async_copy(w1_hbm.at[:, pl.ds(i * W_FC1, W_FC1)], w1.at[i], w1_sem.at[i]) for i in range(N_FC1)]
    w2_copies = [pltpu.make_async_copy(w2_hbm.at[:, pl.ds(i * W_FC2, W_FC2)], w2.at[i], w2_sem.at[i]) for i in range(N_FC2)]

    rows128 = lax.broadcasted_iota(jnp.int32, (128, 256), 0)
    cols256 = lax.broadcasted_iota(jnp.int32, (128, 256), 1)
    diff = cols256 - rows128 % 16

    def build_sel(i, carry):
        sel[pl.ds(pl.multiple_of(i * 128, 128), 128), :] = jnp.where(diff == i * 16, 1.0, 0.0).astype(BF16)
        return carry
    lax.fori_loop(0, 16, build_sel, 0)

    small_copies[0].wait()
    keep = lax.broadcasted_iota(jnp.int32, (8, 128), 1) // 16 == lax.broadcasted_iota(jnp.int32, (8, 128), 0)

    def spread(n, carry):
        base = pl.multiple_of(n * BLOCK, BLOCK)
        for g in range(48):
            p, c = g // 3, g % 3
            t, col = g // 16, (g % 16) * 128
            for py in range(2):
                row = img[n, c, pl.ds(py * 16 + p, 1), :]
                halves = [jnp.where(keep, jnp.broadcast_to(row[:, i * 128:(i + 1) * 128], (8, 128)), 0.0) for i in range(2)]
                lhs[t, pl.ds(base + py * 16, 16), pl.ds(col, 128)] = jnp.concatenate(halves, axis=0).astype(BF16)
        return carry
    lax.fori_loop(0, IMAGES, spread, 0)
    for t in range(3):
        pix[:, t * 256:(t + 1) * 256] = jnp.dot(lhs[t], sel[...], preferred_element_type=F32).astype(BF16)

    for c in small_copies[1:]:
        c.wait()
    bq_copy.wait()
    for c in wq_copies + wo_copies + w1_copies + w2_copies:
        c.start()

    bp_row = as_row(vecs[0])
    for n in range(4):
        cols = slice(n * 256, (n + 1) * 256)
        emb = jnp.dot(pix[...], wp[:, cols], preferred_element_type=F32) + bp_row[:, cols]
        emb = emb.reshape(IMAGES, BLOCK, 256) + pos[:, cols].astype(F32)[None]
        xs[:, cols] = emb.reshape(OWN, 256).astype(BF16)

    pl.semaphore_wait(barrier, 7)

    def block_rows(slot, k, other):
        if slot == 0:
            first = k + 4 * other
        else:
            first = 8 + (k // 2) + 2 * other + 4 * (k % 2)
        return pl.ds(first * BLOCK, BLOCK)

    def x_block(chip_to, slot):
        image = chip_to if slot == 0 else 4 + chip_to // 2
        return xs.at[pl.ds(pl.multiple_of(image * BLOCK, BLOCK), BLOCK), :]

    sends = []
    for k in (3, 1, 2):
        to = chip_at(k)
        for slot in range(2):
            sends.append(remote(x_block(to, slot), xg.at[block_rows(slot, k, 0), :], xsend.at[k - 1, slot], xrecv.at[k - 1, slot], to * 2 + core))
            sends[-1].start()
    for slot in range(2):
        sends.append(remote(x_block(chip, slot), xg.at[block_rows(slot, 0, 1), :], fsend.at[0, slot], frecv.at[0, slot], mate))
        sends[-1].start()
    xg[block_rows(0, 0, 0), :] = xs[pl.ds(pl.multiple_of(chip * BLOCK, BLOCK), BLOCK), :]
    xg[block_rows(1, 0, 0), :] = xs[pl.ds(pl.multiple_of((4 + cy) * BLOCK, BLOCK), BLOCK), :]

    g1_row, c1_row = as_row(vecs[1]), as_row(vecs[2])

    def norm_block(rows):
        y1[rows, :] = norm_rows(xg[rows, :].astype(F32), g1_row, c1_row).astype(BF16)

    def forwarded(slot, k):
        ref = xg.at[block_rows(slot, k, 1), :]
        return remote(ref, ref, fsend.at[k, slot], frecv.at[k, slot], mate)

    for slot in range(2):
        norm_block(block_rows(slot, 0, 0))
    for slot in range(2):
        forwarded(slot, 0).wait_recv()
        norm_block(block_rows(slot, 0, 1))
    for k in (1, 2, 3):
        for slot in range(2):
            ref = xg.at[block_rows(slot, k, 0), :]
            remote(ref, ref, xsend.at[k - 1, slot], xrecv.at[k - 1, slot], chip_at(k) * 2 + core).wait_recv()
            sends.append(remote(ref, xg.at[block_rows(slot, k, 1), :], fsend.at[k, slot], frecv.at[k, slot], mate))
            sends[-1].start()
        for slot in range(2):
            norm_block(block_rows(slot, k, 0))
    for k in (1, 2, 3):
        for slot in range(2):
            forwarded(slot, k).wait_recv()
            norm_block(block_rows(slot, k, 1))

    for c in wq_copies:
        c.wait()
    brow = [as_row(bqkv[t]) for t in range(3)]
    for n in range(2):
        cols = slice(n * 256, (n + 1) * 256)
        qh[:, cols] = (lax.dot_general(y1[0:384, :], wqkv[0, cols, :], NT, preferred_element_type=F32) + brow[0][:, cols]).astype(BF16)
        kh[:, cols] = (lax.dot_general(y1[...], wqkv[1, cols, :], NT, preferred_element_type=F32) + brow[1][:, cols]).astype(BF16)
        vh[:, cols] = (lax.dot_general(y1[...], wqkv[2, cols, :], NT, preferred_element_type=F32) + brow[2][:, cols]).astype(BF16)

    def attend(q0, rows, k0):
        low = lax.broadcasted_iota(jnp.int32, (rows, 128), 1) < 64
        for pair in range(4):
            cols = slice(pair * 128, (pair + 1) * 128)
            q_pair = qh[q0:q0 + rows, cols]
            k_pair = kh[k0:k0 + 256, cols]
            v_pair = vh[k0:k0 + 256, cols]
            heads = []
            for h in range(2):
                q_one = jnp.where(low == (h == 0), q_pair, jnp.zeros_like(q_pair))
                s = lax.dot_general(q_one, k_pair, NT, preferred_element_type=F32)
                e = jnp.exp2((s - jnp.max(s, axis=-1, keepdims=True)) * EXP_SCALE)
                w = (e * (1.0 / jnp.sum(e, axis=-1, keepdims=True))).astype(BF16)
                heads.append(jnp.dot(w, v_pair, preferred_element_type=F32))
            og[q0:q0 + rows, cols] = jnp.where(low, heads[0], heads[1]).astype(BF16)

    o_parts = ((128, 0, 128), (320, 128, 64))

    def o_send(i):
        src, dst, rows = o_parts[i]
        return remote(og.at[pl.ds(src, rows), :], op.at[pl.ds(dst, rows), :], osend.at[i], orecv.at[i], mate)

    attend(128, 128, 0)
    sends.append(o_send(0))
    sends[-1].start()
    attend(256, 128, 256)
    sends.append(o_send(1))
    sends[-1].start()
    attend(0, 128, 0)

    for c in wo_copies:
        c.wait()
    bo_row = as_row(vecs[3])
    res[0:128, :] = xg[0:128, :].astype(F32) + jnp.dot(og[0:128, :], wo[0], preferred_element_type=F32)
    res[128:192, :] = xg[256:320, :].astype(F32) + jnp.dot(og[256:320, :], wo[0], preferred_element_type=F32)
    for i in range(2):
        o_send(i).wait_recv()
    res[...] = res[...] + jnp.dot(op[...], wo[1], preferred_element_type=F32) + bo_row

    g2_row, c2_row = as_row(vecs[4]), as_row(vecs[5])
    for i in range(6):
        rows = slice(i * BLOCK, (i + 1) * BLOCK)
        y2[rows, :] = norm_rows(res[rows, :], g2_row, c2_row).astype(BF16)

    for i in range(N_FC1):
        b1row[i] = as_row(b1[i * 4:(i + 1) * 4, :])
    for c in w1_copies:
        c.wait()

    def fc1_step(i, carry):
        hid[i] = jax.nn.gelu(jnp.dot(y2[...], w1[i], preferred_element_type=F32) + b1row[i], approximate=True).astype(BF16)
        return carry
    lax.fori_loop(0, N_FC1, fc1_step, 0)

    for c in w2_copies:
        c.wait()
    b2_row = as_row(vecs[6])

    homes = ((0, 0), (0, 1), (0, 2), (0, 3), (1, 0), (1, 2))

    def home_copy(j, b, recv):
        slot, k = homes[b]
        other = chip_at(k)
        owner = other if recv else chip
        image = owner if slot == 0 else 4 + owner // 2
        src = outs.at[j, pl.ds(b * BLOCK, BLOCK), :]
        dst = out_hbm.at[image, :, pl.ds(j * W_FC2, W_FC2)]
        if k == 0:
            return pltpu.make_async_copy(src, dst, rsend.at[j, b])
        return remote(src, dst, rsend.at[j, b], rrecv.at[j, b], other * 2 + core)

    keeps = []
    for j in range(N_FC2):
        cols = slice(j * W_FC2, (j + 1) * W_FC2)
        acc = res[:, cols] + b2_row[:, cols]
        for i in range(N_FC1):
            acc = acc + jnp.dot(hid[i], w2[j, i * W_FC1:(i + 1) * W_FC1, :], preferred_element_type=F32)
        outs[j] = acc.astype(BF16)
        for b in (3, 1, 2, 5, 0, 4):
            copy = home_copy(j, b, False)
            copy.start()
            (keeps if homes[b][1] == 0 else sends).append(copy)

    for j in range(N_FC2):
        for b in (1, 2, 5, 3):
            home_copy(j, b, True).wait_recv()
    for c in keeps:
        c.wait()
    for c in sends:
        c.wait_send()


def solution(mesh):
    def device_step(images, w_patch, b_patch, pos_embed, ln1_gain, ln1_bias, w_qkv, b_qkv, w_out, b_out, ln2_gain, ln2_bias, w_fc1, b_fc1, w_fc2, b_fc2):
        tile = lambda v: v.reshape(-1, 128)
        args = (
            jnp.transpose(images, (0, 3, 1, 2)),
            jnp.transpose(w_patch, (0, 2, 1, 3)).reshape(768, D),
            tile(b_patch), pos_embed, tile(ln1_gain), tile(ln1_bias),
            jnp.transpose(w_qkv, (1, 2, 3, 0)).reshape(3 * D, D),
            b_qkv, w_out.reshape(D, D), tile(b_out), tile(ln2_gain), tile(ln2_bias),
            w_fc1, tile(b_fc1), w_fc2, tile(b_fc2))
        vm = pltpu.VMEM
        dma = pltpu.SemaphoreType.DMA
        return pl.pallas_call(
            layer_kernel,
            out_shape=jax.ShapeDtypeStruct((IMAGES, BLOCK, D), BF16),
            in_specs=[pl.BlockSpec(memory_space=pl.ANY)] * len(args),
            out_specs=pl.BlockSpec(memory_space=pl.ANY),
            scratch_shapes=[
                vm((IMAGES, 3, BLOCK, 256), F32), vm((768, D), BF16), vm((BLOCK, D), BF16), vm((7, 8, 128), F32),
                vm((32, 128), F32), vm((3, 8, 64), F32), vm((3, 512, D), BF16), vm((2, 512, D), BF16),
                vm((N_FC1, D, W_FC1), BF16), vm((N_FC2, FF, W_FC2), BF16),
                vm((3, OWN, 2048), BF16), vm((2048, 256), BF16), vm((OWN, 768), BF16), vm((OWN, D), BF16),
                vm((2 * TOKENS, D), BF16), vm((2 * TOKENS, D), BF16),
                vm((384, 512), BF16), vm((512, 512), BF16), vm((512, 512), BF16), vm((384, 512), BF16), vm((OWN, 512), BF16),
                vm((OWN, D), F32), vm((OWN, D), BF16), vm((N_FC1, OWN, W_FC1), BF16), vm((N_FC2, OWN, W_FC2), BF16),
                vm((N_FC1, 1, W_FC1), F32),
                dma((12,)), dma((3,)), dma((2,)), dma((N_FC1,)), dma((N_FC2,)),
                dma((3, 2)), dma((3, 2)), dma((4, 2)), dma((4, 2)), dma((2,)), dma((2,)), dma((N_FC2, 6)), dma((N_FC2, 6)),
            ],
            compiler_params=pltpu.CompilerParams(
                collective_id=0, has_side_effects=True, vmem_limit_bytes=60 * 1024 * 1024),
        )(*args)

    in_specs = (P('dp', 'sp', None, None), P(), P(), P('sp', None), P(), P(), P(), P(), P(), P(), P(), P(), P(), P(), P(), P())
    return jax.shard_map(device_step, mesh=mesh, in_specs=in_specs, out_specs=P('dp', 'sp', None), check_vma=False)
```

time: 182 us -> 35.1 us (0.19)
  waiting for transfers between devices: 71.4 us -> 0 us
  matrix products: 50.6 us -> 0 us
  local copies, waits for them, and re-layouts: 43.3 us -> 1.78 us
  Pallas kernels: 0 us -> 33.1 us
  between operations: 13.6 us -> 0.01 us
  other arithmetic: 2.55 us -> 0 us
    all_gather x1 -> x0, waiting for transfers between devices: 71.4 us -> none  [device_step(): key_value = lax.all_gather(qkv_proj[:, :, 1:], 'sp', axis=1, tiled=True)]
    dot_general x10 -> x0, matrix products: 41.5 us -> none  [the longest x6 17.5 us: one_group(): jnp.einsum('hqk,khe->qhe', att_weights, v_img, preferred_element_type=jnp...]
    pallas_call x0 -> x1, Pallas kernels: none -> 33.1 us  [device_step(): pl.pallas_call(layer_kernel, out_shape=jax.ShapeDtypeStruct((IMAGES, BLOC...]
    while x2 -> x0, local copies, waits for them, and re-layouts: 13.4 us -> none  [attend(): return lax.map(one_image, (queries, keys_all, values_all))]
    squeeze x2 -> x0, local copies, waits for them, and re-layouts: 12.7 us -> none  [device_step(): attended = attend(qkv_proj[:, :, 0], key_value[:, :, 0], key_value[:, :, 1])]
    dot_general x2 -> x0, local copies, waits for them, and re-layouts: 10.7 us -> none  [embed_tokens(): jnp.einsum('bypxqc,pqcd->byxd', pixels, w_patch, preferred_element_type=j...]
    sub x6 -> x0, matrix products: 9.05 us -> none  [one_group(): att_weights = jax.nn.softmax(scores, axis=-1).astype(jnp.bfloat16)]
    reshape x1 -> x0, local copies, waits for them, and re-layouts: 2.68 us -> none  [embed_tokens(): images.astype(jnp.bfloat16)]
  transfers between devices with their start and end apart: 1 -> 0, of which waited for: 1 -> 0; matrix products, arithmetic and copies ran while one was open for 1% -> 0% of each run, Pallas kernels for 0% -> 0%
where the time goes in v1:
time: 35.1 us; the launch traced here: 34.9 us
  Pallas kernels  33.1 us (94%)
  local copies, waits for them, and re-layouts  1.78 us (5%)
    pallas_call x1, Pallas kernels, device_step(): pl.pallas_call(layer_kernel, out_shape=jax.ShapeDtypeStruct((IMAGES, BLOC...  33.1 us
    unnamed x1, local copies, waits for them, and re-layouts  1.78 us

profile of v1, /device:TPU:0, one launch (start us, length us, event | category | flops | bytes accessed | tf_op | source)
XLA Modules:
  0.0 34.9 jit_solution(6330200145636600066)
XLA Ops:
  0.0 33.1 %shard_map.154 = bf16[6,32,1024]{2,1,0:T(8,128)(2,1)} custom-call(f32[6,3,32,256]{3,2,1,0:T(8,128)} %bitcast.19, bf16[768,1024]{1,0:T(8,128)(2,1)} %bitcast.18, f32[8,128]{1,0:T(8,128)} %bitcast.21, bf16[32,1024]{1,0:T(8,128)(2,1)} %pos_hbm.1, f32[8,128]{1,0:T(8,128)} %bitcast.22, f32[8,128]{1,0:T(8,128)} %bitcast.23, bf16[3072,1024]{1,0:T(8,128)(2,1)} %bitcast.16, ...), custom_call_target="tpu_custom_call" | custom-call | tf_op jit(solution)/shard_map/pallas_call | solution.py:285
  33.1 1.8 %copy.18 = bf16[6,32,1024]{2,1,0:T(8,128)(2,1)} copy(bf16[6,32,1024]{2,1,0:T(8,128)(2,1)} %shard_map.154) | data formatting | bytes 786432

commit v2 on v1

--- a/solution.py
+++ b/solution.py
@@ -38,7 +38,7 @@
         w1_hbm, b1_hbm, w2_hbm, b2_hbm,
         out_hbm,
         img, wp, pos, vecs, b1, bqkv, wqkv, wo, w1, w2,
-        lhs, sel, pix, xs, xg, y1, qh, kh, vh, og, op, res, y2, hid, outs, b1row,
+        lhs, sel, pix, xs, xg, y1, qh, kh, vh, og, op, res, y2, hid, outs, b1row, pre,
         in_sem, wqkv_sem, wo_sem, w1_sem, w2_sem,
         xsend, xrecv, fsend, frecv, osend, orecv, rsend, rrecv):
     dp = lax.axis_index("dp")
@@ -172,11 +172,9 @@
     for c in wq_copies:
         c.wait()
     brow = [as_row(bqkv[t]) for t in range(3)]
-    for n in range(2):
-        cols = slice(n * 256, (n + 1) * 256)
-        qh[:, cols] = (lax.dot_general(y1[0:384, :], wqkv[0, cols, :], NT, preferred_element_type=F32) + brow[0][:, cols]).astype(BF16)
-        kh[:, cols] = (lax.dot_general(y1[...], wqkv[1, cols, :], NT, preferred_element_type=F32) + brow[1][:, cols]).astype(BF16)
-        vh[:, cols] = (lax.dot_general(y1[...], wqkv[2, cols, :], NT, preferred_element_type=F32) + brow[2][:, cols]).astype(BF16)
+    qh[...] = (lax.dot_general(y1[0:384, :], wqkv[0], NT, preferred_element_type=F32) + brow[0]).astype(BF16)
+    kh[...] = (lax.dot_general(y1[...], wqkv[1], NT, preferred_element_type=F32) + brow[1]).astype(BF16)
+    vh[...] = (lax.dot_general(y1[...], wqkv[2], NT, preferred_element_type=F32) + brow[2]).astype(BF16)
 
     def attend(q0, rows, k0):
         low = lax.broadcasted_iota(jnp.int32, (rows, 128), 1) < 64
@@ -227,10 +225,14 @@
     for c in w1_copies:
         c.wait()
 
-    def fc1_step(i, carry):
-        hid[i] = jax.nn.gelu(jnp.dot(y2[...], w1[i], preferred_element_type=F32) + b1row[i], approximate=True).astype(BF16)
-        return carry
-    lax.fori_loop(0, N_FC1, fc1_step, 0)
+    def activate(i):
+        hid[:, i * W_FC1:(i + 1) * W_FC1] = jax.nn.gelu(pre[i % 2], approximate=True).astype(BF16)
+
+    for i in range(N_FC1):
+        pre[i % 2] = jnp.dot(y2[...], w1[i], preferred_element_type=F32) + b1row[i]
+        if i:
+            activate(i - 1)
+    activate(N_FC1 - 1)
 
     for c in w2_copies:
         c.wait()
@@ -252,10 +254,8 @@
     keeps = []
     for j in range(N_FC2):
         cols = slice(j * W_FC2, (j + 1) * W_FC2)
-        acc = res[:, cols] + b2_row[:, cols]
-        for i in range(N_FC1):
-            acc = acc + jnp.dot(hid[i], w2[j, i * W_FC1:(i + 1) * W_FC1, :], preferred_element_type=F32)
-        outs[j] = acc.astype(BF16)
+        parts = [jnp.dot(hid[:, i:i + FF // 2], w2[j, i:i + FF // 2, :], preferred_element_type=F32) for i in (0, FF // 2)]
+        outs[j] = (parts[0] + parts[1] + (res[:, cols] + b2_row[:, cols])).astype(BF16)
         for b in (3, 1, 2, 5, 0, 4):
             copy = home_copy(j, b, False)
             copy.start()
@@ -294,8 +294,8 @@
                 vm((3, OWN, 2048), BF16), vm((2048, 256), BF16), vm((OWN, 768), BF16), vm((OWN, D), BF16),
                 vm((2 * TOKENS, D), BF16), vm((2 * TOKENS, D), BF16),
                 vm((384, 512), BF16), vm((512, 512), BF16), vm((512, 512), BF16), vm((384, 512), BF16), vm((OWN, 512), BF16),
-                vm((OWN, D), F32), vm((OWN, D), BF16), vm((N_FC1, OWN, W_FC1), BF16), vm((N_FC2, OWN, W_FC2), BF16),
-                vm((N_FC1, 1, W_FC1), F32),
+                vm((OWN, D), F32), vm((OWN, D), BF16), vm((OWN, FF), BF16), vm((N_FC2, OWN, W_FC2), BF16),
+                vm((N_FC1, 1, W_FC1), F32), vm((2, OWN, W_FC1), F32),
                 dma((12,)), dma((3,)), dma((2,)), dma((N_FC1,)), dma((N_FC2,)),
                 dma((3, 2)), dma((3, 2)), dma((4, 2)), dma((4, 2)), dma((2,)), dma((2,)), dma((N_FC2, 6)), dma((N_FC2, 6)),
             ],

time: 35.1 us -> 33.2 us (0.946)
  Pallas kernels: 33.1 us -> 31.2 us
    pallas_call x1, Pallas kernels: 33.1 us -> 31.2 us  [device_step(): pl.pallas_call(layer_kernel, out_shape=jax.ShapeDtypeStruct((IMAGES, BLOC...]
where the time goes in v2:
time: 33.2 us; the launch traced here: 33 us
  Pallas kernels  31.2 us (94%)
  local copies, waits for them, and re-layouts  1.78 us (5%)
    pallas_call x1, Pallas kernels, device_step(): pl.pallas_call(layer_kernel, out_shape=jax.ShapeDtypeStruct((IMAGES, BLOC...  31.2 us
    unnamed x1, local copies, waits for them, and re-layouts  1.78 us

profile of v2, /device:TPU:0, one launch (start us, length us, event | category | flops | bytes accessed | tf_op | source)
XLA Modules:
  0.0 33.0 jit_solution(12757633087266501871)
XLA Ops:
  0.0 31.2 %shard_map.154 = bf16[6,32,1024]{2,1,0:T(8,128)(2,1)} custom-call(f32[6,3,32,256]{3,2,1,0:T(8,128)} %bitcast.19, bf16[768,1024]{1,0:T(8,128)(2,1)} %bitcast.18, f32[8,128]{1,0:T(8,128)} %bitcast.21, bf16[32,1024]{1,0:T(8,128)(2,1)} %pos_hbm.1, f32[8,128]{1,0:T(8,128)} %bitcast.22, f32[8,128]{1,0:T(8,128)} %bitcast.23, bf16[3072,1024]{1,0:T(8,128)(2,1)} %bitcast.16, ...), custom_call_target="tpu_custom_call" | custom-call | tf_op jit(solution)/shard_map/pallas_call | solution.py:285
  31.2 1.8 %copy.18 = bf16[6,32,1024]{2,1,0:T(8,128)(2,1)} copy(bf16[6,32,1024]{2,1,0:T(8,128)(2,1)} %shard_map.154) | data formatting | bytes 786432

commit v3 on v2

v3 whole, which is shorter than its diff:
```python
import functools
import math
import jax
import jax.numpy as jnp
from jax import lax
from jax.experimental import pallas as pl
from jax.experimental.pallas import tpu as pltpu
from jax.sharding import PartitionSpec as P

LN_EPS = 1e-6
F32 = jnp.float32
BF16 = jnp.bfloat16
D = 1024
FF = 4096
IMAGES = 6
BLOCK = 32
TOKENS = 256
OWN = 192
HALF = 96
N_FC1, W_FC1 = 8, 512
N_FC2, W_FC2 = 2, 512
EXP_SCALE = math.log2(math.e) / 8.0
MESH = pl.DeviceIdType.MESH
NT = (((1,), (1,)), ((), ()))


def as_row(vec):
    return jnp.concatenate([vec[i:i + 1, :] for i in range(vec.shape[0])], axis=1)


def norm_rows(x_in, gain, bias):
    centered = x_in - jnp.mean(x_in, axis=-1, keepdims=True)
    variance = jnp.mean(centered * centered, axis=-1, keepdims=True)
    return centered * lax.rsqrt(variance + LN_EPS) * gain + bias


def layer_kernel(
        img_hbm, wp_hbm, bp_hbm, pos_hbm, g1_hbm, c1_hbm, wqkv_hbm, bqkv_hbm, wo_hbm, bo_hbm, g2_hbm, c2_hbm,
        w1_hbm, b1_hbm, w2_hbm, b2_hbm,
        out_hbm,
        img, wp, pos, vecs, b1, bqkv, wqkv, wo, w1, w2,
        lhs, sel, pix, xs, xg, y1, qh, kh, vh, og, op, oh, res, y2, hid, outs, b1row, pre,
        in_sem, wqkv_sem, wo_sem, w1_sem, w2_sem,
        xsend, xrecv, fsend, frecv, osend, orecv, hsend, hrecv, rsend, rrecv, keep_sem):
    dp = lax.axis_index("dp")
    me = lax.axis_index("sp")
    chip = me // 2
    core = me % 2
    mate = chip * 2 + (1 - core)
    cx = chip % 2
    cy = chip // 2

    def remote(src, dst, ssem, rsem, dev):
        return pltpu.make_async_remote_copy(
            src_ref=src, dst_ref=dst, send_sem=ssem, recv_sem=rsem, device_id=(dp, dev), device_id_type=MESH)

    def chip_at(k):
        return ((cy + k // 2) % 2) * 2 + (cx + k % 2) % 2

    barrier = pltpu.get_barrier_semaphore()
    for k in range(1, 8):
        pl.semaphore_signal(barrier, inc=1, device_id=(dp, (me + k) % 8), device_id_type=MESH)

    groups = ((4, 2), (0, 4))
    small = [(img_hbm.at[pl.ds(n0, n), :, :, :], img.at[pl.ds(n0, n), :, :, :]) for n0, n in groups] + [(wp_hbm, wp), (pos_hbm, pos)]
    for i, v in enumerate((bp_hbm, g1_hbm, c1_hbm, bo_hbm, g2_hbm, c2_hbm, b2_hbm)):
        small.append((v, vecs.at[i]))
    small.append((b1_hbm, b1))
    small.append((bqkv_hbm.at[:, pl.ds(pl.multiple_of(core * 8, 8), 8), :], bqkv))
    small_copies = [pltpu.make_async_copy(s, d, in_sem.at[i]) for i, (s, d) in enumerate(small)]
    for i in (0, 2, 1) + tuple(range(3, len(small))):
        small_copies[i].start()
    wq_copies = [
        pltpu.make_async_copy(wqkv_hbm.at[pl.ds(pl.multiple_of(t * D + core * 512, 512), 512), :], wqkv.at[t], wqkv_sem.at[t])
        for t in range(3)]
    wo_copies = [
        pltpu.make_async_copy(wo_hbm.at[pl.ds(pl.multiple_of(((core + i) % 2) * 512, 512), 512), :], wo.at[i], wo_sem.at[i])
        for i in range(2)]
    w1_copies = [pltpu.make_async_copy(w1_hbm.at[:, pl.ds(i * W_FC1, W_FC1)], w1.at[i], w1_sem.at[i]) for i in range(N_FC1)]
    w2_copies = [pltpu.make_async_copy(w2_hbm.at[:, pl.ds(i * W_FC2, W_FC2)], w2.at[i], w2_sem.at[i]) for i in range(N_FC2)]

    rows128 = lax.broadcasted_iota(jnp.int32, (128, 256), 0)
    cols256 = lax.broadcasted_iota(jnp.int32, (128, 256), 1)
    diff = cols256 - rows128 % 16

    def build_sel(i, carry):
        sel[pl.ds(pl.multiple_of(i * 128, 128), 128), :] = jnp.where(diff == i * 16, 1.0, 0.0).astype(BF16)
        return carry
    lax.fori_loop(0, 16, build_sel, 0)

    keep = lax.broadcasted_iota(jnp.int32, (8, 128), 1) // 16 == lax.broadcasted_iota(jnp.int32, (8, 128), 0)

    def embed(group):
        n0, count = groups[group]
        m = count * BLOCK
        top = n0 * BLOCK * 3

        def spread(i, carry):
            for g in range(48):
                p, c = g // 3, g % 3
                t, col = g // 16, (g % 16) * 128
                for py in range(2):
                    row = img[n0 + i, c, pl.ds(py * 16 + p, 1), :]
                    halves = [jnp.where(keep, jnp.broadcast_to(row[:, j * 128:(j + 1) * 128], (8, 128)), 0.0) for j in range(2)]
                    at = pl.multiple_of(top + t * m + i * BLOCK + py * 16, 16)
                    lhs[pl.ds(at, 16), pl.ds(col, 128)] = jnp.concatenate(halves, axis=0).astype(BF16)
            return carry
        lax.fori_loop(0, count, spread, 0)
        h = 3 * m // 2
        both = [jnp.dot(lhs[top + i * h:top + (i + 1) * h, :], sel[...], preferred_element_type=F32).astype(BF16) for i in range(2)]
        rows = slice(n0 * BLOCK, n0 * BLOCK + m)
        pix[rows, 0:256] = both[0][0:m]
        pix[rows, 256:512] = jnp.concatenate([both[0][m:], both[1][0:m // 2]], axis=0)
        pix[rows, 512:768] = both[1][m // 2:]
        return rows, count

    def project(rows, count):
        for n in range(2):
            cols = slice(n * 512, (n + 1) * 512)
            emb = jnp.dot(pix[rows, :], wp[:, cols], preferred_element_type=F32) + bp_row[:, cols]
            emb = emb.reshape(count, BLOCK, 512) + pos[:, cols].astype(F32)[None]
            xs[rows, cols] = emb.reshape(count * BLOCK, 512).astype(BF16)

    slot1_first = {3: 8, 1: 10, 0: 12, 2: 13}

    def block(slot, k, other):
        first = 2 * k + other if slot == 0 else slot1_first[k] + other * (2 if k in (0, 2) else 1)
        return pl.ds(first * BLOCK, BLOCK)

    def x_block(chip_to, slot):
        image = chip_to if slot == 0 else 4 + chip_to // 2
        return pl.ds(pl.multiple_of(image * BLOCK, BLOCK), BLOCK)

    sends = []

    def start(copy):
        copy.start()
        sends.append(copy)

    def send_slot(slot):
        for k in (2, 1, 3):
            to = chip_at(k)
            start(remote(xs.at[x_block(to, slot), :], xg.at[block(slot, k, 0), :], xsend.at[k - 1, slot], xrecv.at[k - 1, slot], to * 2 + core))
        start(remote(xs.at[x_block(chip, slot), :], xg.at[block(slot, 0, 1), :], fsend.at[0, slot], frecv.at[0, slot], mate))
        xg[block(slot, 0, 0), :] = xs[x_block(chip, slot), :]

    small_copies[0].wait()
    part = embed(0)
    for c in small_copies[2:]:
        c.wait()
    small_copies[1].wait()
    for c in wq_copies + wo_copies + w1_copies + w2_copies:
        c.start()
    bp_row = as_row(vecs[0])
    project(*part)
    pl.semaphore_wait(barrier, 7)
    send_slot(1)
    project(*embed(1))
    send_slot(0)

    g1_row, c1_row = as_row(vecs[1]), as_row(vecs[2])

    def norm_blocks(blocks):
        for rows in blocks:
            y1[rows, :] = norm_rows(xg[rows, :].astype(F32), g1_row, c1_row).astype(BF16)

    def arrive(slot, k):
        ref = xg.at[block(slot, k, 0), :]
        remote(ref, ref, xsend.at[k - 1, slot], xrecv.at[k - 1, slot], chip_at(k) * 2 + core).wait_recv()
        start(remote(ref, xg.at[block(slot, k, 1), :], fsend.at[k, slot], frecv.at[k, slot], mate))

    def forwarded(slot, k):
        ref = xg.at[block(slot, k, 1), :]
        remote(ref, ref, fsend.at[k, slot], frecv.at[k, slot], mate).wait_recv()

    norm_blocks([block(1, 0, 0), block(0, 0, 0)])
    for slot in (1, 0):
        forwarded(slot, 0)
    norm_blocks([block(1, 0, 1), block(0, 0, 1)])
    for slot in (1, 0):
        for k in (2, 1):
            arrive(slot, k)
        norm_blocks([block(slot, k, 0) for k in (2, 1)])
    for c in wq_copies:
        c.wait()
    brow = [as_row(bqkv[t]) for t in range(3)]
    for slot in (1, 0):
        for k in (2, 1):
            forwarded(slot, k)
    norm_blocks([block(slot, k, 1) for slot in (1, 0) for k in (2, 1)])

    early_q, early_kv = ((0, 192), (384, 512)), ((0, 192), (320, 512))

    def heads_of(t, dst, pieces):
        rows = jnp.concatenate([y1[a:b, :] for a, b in pieces], axis=0)
        got = (lax.dot_general(rows, wqkv[t], NT, preferred_element_type=F32) + brow[t]).astype(BF16)
        at = 0
        for a, b in pieces:
            dst[a:b, :] = got[at:at + b - a]
            at += b - a

    heads_of(0, qh, early_q)
    heads_of(1, kh, early_kv)
    for slot in (1, 0):
        arrive(slot, 3)
    heads_of(2, vh, early_kv)
    norm_blocks([block(slot, 3, 0) for slot in (1, 0)])
    for slot in (1, 0):
        forwarded(slot, 3)
    norm_blocks([block(slot, 3, 1) for slot in (1, 0)])
    heads_of(0, qh, ((192, 256),))
    heads_of(1, kh, ((192, 320),))
    heads_of(2, vh, ((192, 320),))

    def attend(q0, rows, k0):
        low = lax.broadcasted_iota(jnp.int32, (rows, 128), 1) < 64
        for pair in range(4):
            cols = slice(pair * 128, (pair + 1) * 128)
            q_pair = qh[q0:q0 + rows, cols]
            k_pair = kh[k0:k0 + 256, cols]
            v_pair = vh[k0:k0 + 256, cols]
            heads = []
            for h in range(2):
                q_one = jnp.where(low == (h == 0), q_pair, jnp.zeros_like(q_pair))
                s = lax.dot_general(q_one, k_pair, NT, preferred_element_type=F32)
                e = jnp.exp2((s - jnp.max(s, axis=-1, keepdims=True)) * EXP_SCALE)
                w = (e * (1.0 / jnp.sum(e, axis=-1, keepdims=True))).astype(BF16)
                heads.append(jnp.dot(w, v_pair, preferred_element_type=F32))
            og[q0:q0 + rows, cols] = jnp.where(low, heads[0], heads[1]).astype(BF16)

    def o_home(k, other, recv):
        dev = chip_at(k) * 2 + (core if other == 0 else 1 - core)
        return remote(og.at[block(0, k, other), :], oh.at[other, pl.ds((k - 1) * BLOCK, BLOCK), :],
                      hsend.at[k - 1, other], hrecv.at[k - 1, other], dev)

    o_parts = ((32, 0, 32), (448, 32, 64))

    def o_send(i):
        src, dst, rows = o_parts[i]
        return remote(og.at[pl.ds(src, rows), :], op.at[pl.ds(dst, rows), :], osend.at[i], orecv.at[i], mate)

    attend(128, 128, 0)
    for k, other in ((3, 0), (3, 1), (2, 0), (2, 1)):
        start(o_home(k, other, False))
    attend(0, 128, 0)
    start(o_send(0))
    for other in range(2):
        start(o_home(1, other, False))
    attend(384, 128, 256)
    start(o_send(1))

    for c in wo_copies + w1_copies + w2_copies:
        c.wait()
    bo_row, g2_row, c2_row, b2_row = [as_row(vecs[i]) for i in (3, 4, 5, 6)]
    for i in range(N_FC1):
        b1row[i] = as_row(b1[i * 4:(i + 1) * 4, :])

    def finish(x_in, near, far, ready):
        res[...] = x_in.astype(F32) + jnp.dot(near(), wo[0], preferred_element_type=F32)
        ready()
        res[...] = res[...] + jnp.dot(far(), wo[1], preferred_element_type=F32) + bo_row
        for i in range(3):
            rows = slice(i * BLOCK, (i + 1) * BLOCK)
            y2[rows, :] = norm_rows(res[rows, :], g2_row, c2_row).astype(BF16)

        def activate(i):
            hid[:, i * W_FC1:(i + 1) * W_FC1] = jax.nn.gelu(pre[i % 2], approximate=True).astype(BF16)

        for i in range(N_FC1):
            pre[i % 2] = jnp.dot(y2[...], w1[i], preferred_element_type=F32) + b1row[i]
            if i:
                activate(i - 1)
        activate(N_FC1 - 1)

    def second(j):
        cols = slice(j * W_FC2, (j + 1) * W_FC2)
        return (jnp.dot(hid[...], w2[j], preferred_element_type=F32) + (res[:, cols] + b2_row[:, cols])).astype(BF16)

    def mate_ready():
        for i in range(2):
            o_send(i).wait_recv()

    finish(jnp.concatenate([xg[0:32, :], xg[384:448, :]], axis=0),
           lambda: jnp.concatenate([og[0:32, :], og[384:448, :]], axis=0), lambda: op[...], mate_ready)

    def shared_home(j, recv):
        other = chip_at(2)
        image = 4 + (other if recv else chip) // 2
        return remote(outs.at[0, j, pl.ds(64, BLOCK), :], out_hbm.at[image, :, pl.ds(j * W_FC2, W_FC2)],
                      rsend.at[j], rrecv.at[j], other * 2 + core)

    keeps = []

    def keep_rows(half, j, b, image):
        copy = pltpu.make_async_copy(outs.at[half, j, pl.ds(b * BLOCK, BLOCK), :], out_hbm.at[image, :, pl.ds(j * W_FC2, W_FC2)],
                                     keep_sem.at[half, j, b])
        copy.start()
        keeps.append(copy)

    for j in range(N_FC2):
        outs[0, j] = second(j)
        start(shared_home(j, False))
        keep_rows(0, j, 0, chip)
        keep_rows(0, j, 1, 4 + cy)

    def home_ready():
        for k in (1, 2, 3):
            o_home(k, 1, True).wait_recv()

    for k in (1, 2, 3):
        o_home(k, 0, True).wait_recv()
    finish(jnp.concatenate([xs[x_block(chip_at(k), 0), :] for k in (1, 2, 3)], axis=0), lambda: oh[0], lambda: oh[1], home_ready)
    for j in range(N_FC2):
        outs[1, j] = second(j)
        for k in (1, 2, 3):
            keep_rows(1, j, k - 1, chip_at(k))

    for j in range(N_FC2):
        shared_home(j, True).wait_recv()
    for c in keeps:
        c.wait()
    for c in sends:
        c.wait_send()


def solution(mesh):
    def device_step(images, w_patch, b_patch, pos_embed, ln1_gain, ln1_bias, w_qkv, b_qkv, w_out, b_out, ln2_gain, ln2_bias, w_fc1, b_fc1, w_fc2, b_fc2):
        tile = lambda v: v.reshape(-1, 128)
        args = (
            jnp.transpose(images, (0, 3, 1, 2)),
            jnp.transpose(w_patch, (0, 2, 1, 3)).reshape(768, D),
            tile(b_patch), pos_embed, tile(ln1_gain), tile(ln1_bias),
            jnp.transpose(w_qkv, (1, 2, 3, 0)).reshape(3 * D, D),
            b_qkv, w_out.reshape(D, D), tile(b_out), tile(ln2_gain), tile(ln2_bias),
            w_fc1, tile(b_fc1), w_fc2, tile(b_fc2))
        vm = pltpu.VMEM
        dma = pltpu.SemaphoreType.DMA
        return pl.pallas_call(
            layer_kernel,
            out_shape=jax.ShapeDtypeStruct((IMAGES, BLOCK, D), BF16),
            in_specs=[pl.BlockSpec(memory_space=pl.ANY)] * len(args),
            out_specs=pl.BlockSpec(memory_space=pl.ANY),
            scratch_shapes=[
                vm((IMAGES, 3, BLOCK, 256), F32), vm((768, D), BF16), vm((BLOCK, D), BF16), vm((7, 8, 128), F32),
                vm((32, 128), F32), vm((3, 8, 64), F32), vm((3, 512, D), BF16), vm((2, 512, D), BF16),
                vm((N_FC1, D, W_FC1), BF16), vm((N_FC2, FF, W_FC2), BF16),
                vm((3 * OWN, 2048), BF16), vm((2048, 256), BF16), vm((OWN, 768), BF16), vm((OWN, D), BF16),
                vm((2 * TOKENS, D), BF16), vm((2 * TOKENS, D), BF16),
                vm((512, 512), BF16), vm((512, 512), BF16), vm((512, 512), BF16), vm((512, 512), BF16),
                vm((HALF, 512), BF16), vm((2, HALF, 512), BF16),
                vm((HALF, D), F32), vm((HALF, D), BF16), vm((HALF, FF), BF16), vm((2, N_FC2, HALF, W_FC2), BF16),
                vm((N_FC1, 1, W_FC1), F32), vm((2, HALF, W_FC1), F32),
                dma((13,)), dma((3,)), dma((2,)), dma((N_FC1,)), dma((N_FC2,)),
                dma((3, 2)), dma((3, 2)), dma((4, 2)), dma((4, 2)), dma((2,)), dma((2,)), dma((3, 2)), dma((3, 2)),
                dma((N_FC2,)), dma((N_FC2,)), dma((2, N_FC2, 3)),
            ],
            compiler_params=pltpu.CompilerParams(
                collective_id=0, has_side_effects=True, vmem_limit_bytes=60 * 1024 * 1024),
        )(*args)

    in_specs = (P('dp', 'sp', None, None), P(), P(), P('sp', None), P(), P(), P(), P(), P(), P(), P(), P(), P(), P(), P(), P())
    return jax.shard_map(device_step, mesh=mesh, in_specs=in_specs, out_specs=P('dp', 'sp', None), check_vma=False)
```

time: 33.2 us -> 28.6 us (0.86)
  Pallas kernels: 31.2 us -> 26.7 us
    pallas_call x1, Pallas kernels: 31.2 us -> 26.7 us  [device_step(): pl.pallas_call(layer_kernel, out_shape=jax.ShapeDtypeStruct((IMAGES, BLOC...]
where the time goes in v3:
time: 28.6 us; the launch traced here: 28.5 us
  Pallas kernels  26.7 us (93%)
  local copies, waits for them, and re-layouts  1.78 us (6%)
    pallas_call x1, Pallas kernels, device_step(): pl.pallas_call(layer_kernel, out_shape=jax.ShapeDtypeStruct((IMAGES, BLOC...  26.7 us
    unnamed x1, local copies, waits for them, and re-layouts  1.78 us

profile of v3, /device:TPU:0, one launch (start us, length us, event | category | flops | bytes accessed | tf_op | source)
XLA Modules:
  0.0 28.5 jit_solution(14002526093243043672)
XLA Ops:
  0.0 26.7 %shard_map.154 = bf16[6,32,1024]{2,1,0:T(8,128)(2,1)} custom-call(f32[6,3,32,256]{3,2,1,0:T(8,128)} %bitcast.19, bf16[768,1024]{1,0:T(8,128)(2,1)} %bitcast.18, f32[8,128]{1,0:T(8,128)} %bitcast.21, bf16[32,1024]{1,0:T(8,128)(2,1)} %pos_hbm.1, f32[8,128]{1,0:T(8,128)} %bitcast.22, f32[8,128]{1,0:T(8,128)} %bitcast.23, bf16[3072,1024]{1,0:T(8,128)(2,1)} %bitcast.16, ...), custom_call_target="tpu_custom_call" | custom-call | tf_op jit(solution)/shard_map/pallas_call | solution.py:338
  26.7 1.8 %copy.18 = bf16[6,32,1024]{2,1,0:T(8,128)(2,1)} copy(bf16[6,32,1024]{2,1,0:T(8,128)(2,1)} %shard_map.154) | data formatting | bytes 786432

commit v4 on v3

--- a/solution.py
+++ b/solution.py
@@ -16,7 +16,7 @@
 BLOCK = 32
 TOKENS = 256
 OWN = 192
-HALF = 96
+HALF = 128
 N_FC1, W_FC1 = 8, 512
 N_FC2, W_FC2 = 2, 512
 EXP_SCALE = math.log2(math.e) / 8.0
@@ -37,11 +37,11 @@
 def layer_kernel(
         img_hbm, wp_hbm, bp_hbm, pos_hbm, g1_hbm, c1_hbm, wqkv_hbm, bqkv_hbm, wo_hbm, bo_hbm, g2_hbm, c2_hbm,
         w1_hbm, b1_hbm, w2_hbm, b2_hbm,
-        out_hbm,
+        out,
         img, wp, pos, vecs, b1, bqkv, wqkv, wo, w1, w2,
-        lhs, sel, pix, xs, xg, y1, qh, kh, vh, og, op, oh, res, y2, hid, outs, b1row, pre,
+        lhs, sel, pix, xs, xg, y1, qh, kh, vh, og, op, oh, res, y2, hid, back, b1row, pre,
         in_sem, wqkv_sem, wo_sem, w1_sem, w2_sem,
-        xsend, xrecv, fsend, frecv, osend, orecv, hsend, hrecv, rsend, rrecv, keep_sem):
+        xsend, xrecv, fsend, frecv, osend, orecv, hsend, hrecv, rsend, rrecv):
     dp = lax.axis_index("dp")
     me = lax.axis_index("sp")
     chip = me // 2
@@ -228,26 +228,22 @@
                 heads.append(jnp.dot(w, v_pair, preferred_element_type=F32))
             og[q0:q0 + rows, cols] = jnp.where(low, heads[0], heads[1]).astype(BF16)
 
-    def o_home(k, other, recv):
+    def o_home(k, other):
         dev = chip_at(k) * 2 + (core if other == 0 else 1 - core)
-        return remote(og.at[block(0, k, other), :], oh.at[other, pl.ds((k - 1) * BLOCK, BLOCK), :],
-                      hsend.at[k - 1, other], hrecv.at[k - 1, other], dev)
-
-    o_parts = ((32, 0, 32), (448, 32, 64))
-
-    def o_send(i):
-        src, dst, rows = o_parts[i]
-        return remote(og.at[pl.ds(src, rows), :], op.at[pl.ds(dst, rows), :], osend.at[i], orecv.at[i], mate)
+        return remote(og.at[block(0, k, other), :], oh.at[other, pl.ds(k * BLOCK, BLOCK), :],
+                      hsend.at[k, other], hrecv.at[k, other], dev)
+
+    o_mate = remote(og.at[pl.ds(448, 64), :], op, osend, orecv, mate)
 
     attend(128, 128, 0)
-    for k, other in ((3, 0), (3, 1), (2, 0), (2, 1)):
-        start(o_home(k, other, False))
+    for k in (3, 2):
+        for other in range(2):
+            start(o_home(k, other))
+    attend(384, 128, 256)
+    start(o_mate)
     attend(0, 128, 0)
-    start(o_send(0))
-    for other in range(2):
-        start(o_home(1, other, False))
-    attend(384, 128, 256)
-    start(o_send(1))
+    for k, other in ((1, 0), (1, 1), (0, 1)):
+        start(o_home(k, other))
 
     for c in wo_copies + w1_copies + w2_copies:
         c.wait()
@@ -255,70 +251,54 @@
     for i in range(N_FC1):
         b1row[i] = as_row(b1[i * 4:(i + 1) * 4, :])
 
-    def finish(x_in, near, far, ready):
-        res[...] = x_in.astype(F32) + jnp.dot(near(), wo[0], preferred_element_type=F32)
+    def finish(m, x_in, near, far, ready):
+        res[0:m, :] = x_in.astype(F32) + jnp.dot(near, wo[0], preferred_element_type=F32)
         ready()
-        res[...] = res[...] + jnp.dot(far(), wo[1], preferred_element_type=F32) + bo_row
-        for i in range(3):
+        res[0:m, :] = res[0:m, :] + jnp.dot(far[...], wo[1], preferred_element_type=F32) + bo_row
+        for i in range(m // BLOCK):
             rows = slice(i * BLOCK, (i + 1) * BLOCK)
             y2[rows, :] = norm_rows(res[rows, :], g2_row, c2_row).astype(BF16)
 
         def activate(i):
-            hid[:, i * W_FC1:(i + 1) * W_FC1] = jax.nn.gelu(pre[i % 2], approximate=True).astype(BF16)
+            hid[0:m, i * W_FC1:(i + 1) * W_FC1] = jax.nn.gelu(pre[i % 2, 0:m], approximate=True).astype(BF16)
 
         for i in range(N_FC1):
-            pre[i % 2] = jnp.dot(y2[...], w1[i], preferred_element_type=F32) + b1row[i]
+            pre[i % 2, 0:m] = jnp.dot(y2[0:m, :], w1[i], preferred_element_type=F32) + b1row[i]
             if i:
                 activate(i - 1)
         activate(N_FC1 - 1)
 
-    def second(j):
+    def second(m, j):
         cols = slice(j * W_FC2, (j + 1) * W_FC2)
-        return (jnp.dot(hid[...], w2[j], preferred_element_type=F32) + (res[:, cols] + b2_row[:, cols])).astype(BF16)
-
-    def mate_ready():
-        for i in range(2):
-            o_send(i).wait_recv()
-
-    finish(jnp.concatenate([xg[0:32, :], xg[384:448, :]], axis=0),
-           lambda: jnp.concatenate([og[0:32, :], og[384:448, :]], axis=0), lambda: op[...], mate_ready)
+        return (jnp.dot(hid[0:m, :], w2[j], preferred_element_type=F32) + (res[0:m, cols] + b2_row[:, cols])).astype(BF16)
 
     def shared_home(j, recv):
         other = chip_at(2)
         image = 4 + (other if recv else chip) // 2
-        return remote(outs.at[0, j, pl.ds(64, BLOCK), :], out_hbm.at[image, :, pl.ds(j * W_FC2, W_FC2)],
-                      rsend.at[j], rrecv.at[j], other * 2 + core)
-
-    keeps = []
-
-    def keep_rows(half, j, b, image):
-        copy = pltpu.make_async_copy(outs.at[half, j, pl.ds(b * BLOCK, BLOCK), :], out_hbm.at[image, :, pl.ds(j * W_FC2, W_FC2)],
-                                     keep_sem.at[half, j, b])
-        copy.start()
-        keeps.append(copy)
-
+        return remote(back.at[j], out.at[image, :, pl.ds(j * W_FC2, W_FC2)], rsend.at[j], rrecv.at[j], other * 2 + core)
+
+    finish(64, xg[384:448, :], og[384:448, :], op, o_mate.wait_recv)
     for j in range(N_FC2):
-        outs[0, j] = second(j)
+        rows = second(64, j)
+        back[j] = rows[BLOCK:]
         start(shared_home(j, False))
-        keep_rows(0, j, 0, chip)
-        keep_rows(0, j, 1, 4 + cy)
+        out[4 + cy, :, j * W_FC2:(j + 1) * W_FC2] = rows[0:BLOCK]
 
     def home_ready():
-        for k in (1, 2, 3):
-            o_home(k, 1, True).wait_recv()
+        for k in range(4):
+            o_home(k, 1).wait_recv()
 
     for k in (1, 2, 3):
-        o_home(k, 0, True).wait_recv()
-    finish(jnp.concatenate([xs[x_block(chip_at(k), 0), :] for k in (1, 2, 3)], axis=0), lambda: oh[0], lambda: oh[1], home_ready)
+        o_home(k, 0).wait_recv()
+    finish(128, jnp.concatenate([xg[0:32, :]] + [xs[x_block(chip_at(k), 0), :] for k in (1, 2, 3)], axis=0),
+           jnp.concatenate([og[0:32, :], oh[0, 32:128, :]], axis=0), oh.at[1], home_ready)
     for j in range(N_FC2):
-        outs[1, j] = second(j)
-        for k in (1, 2, 3):
-            keep_rows(1, j, k - 1, chip_at(k))
+        rows = second(128, j)
+        for k in range(4):
+            out[chip_at(k), :, j * W_FC2:(j + 1) * W_FC2] = rows[k * BLOCK:(k + 1) * BLOCK]
 
     for j in range(N_FC2):
         shared_home(j, True).wait_recv()
-    for c in keeps:
-        c.wait()
     for c in sends:
         c.wait_send()
 
@@ -337,9 +317,9 @@
         dma = pltpu.SemaphoreType.DMA
         return pl.pallas_call(
             layer_kernel,
-            out_shape=jax.ShapeDtypeStruct((IMAGES, BLOCK, D), BF16),
+            out_shape=pltpu.VMEM((IMAGES, BLOCK, D), BF16),
             in_specs=[pl.BlockSpec(memory_space=pl.ANY)] * len(args),
-            out_specs=pl.BlockSpec(memory_space=pl.ANY),
+            out_specs=pl.BlockSpec(memory_space=pltpu.VMEM),
             scratch_shapes=[
                 vm((IMAGES, 3, BLOCK, 256), F32), vm((768, D), BF16), vm((BLOCK, D), BF16), vm((7, 8, 128), F32),
                 vm((32, 128), F32), vm((3, 8, 64), F32), vm((3, 512, D), BF16), vm((2, 512, D), BF16),
@@ -347,12 +327,12 @@
                 vm((3 * OWN, 2048), BF16), vm((2048, 256), BF16), vm((OWN, 768), BF16), vm((OWN, D), BF16),
                 vm((2 * TOKENS, D), BF16), vm((2 * TOKENS, D), BF16),
                 vm((512, 512), BF16), vm((512, 512), BF16), vm((512, 512), BF16), vm((512, 512), BF16),
-                vm((HALF, 512), BF16), vm((2, HALF, 512), BF16),
-                vm((HALF, D), F32), vm((HALF, D), BF16), vm((HALF, FF), BF16), vm((2, N_FC2, HALF, W_FC2), BF16),
+                vm((64, 512), BF16), vm((2, HALF, 512), BF16),
+                vm((HALF, D), F32), vm((HALF, D), BF16), vm((HALF, FF), BF16), vm((N_FC2, BLOCK, W_FC2), BF16),
                 vm((N_FC1, 1, W_FC1), F32), vm((2, HALF, W_FC1), F32),
                 dma((13,)), dma((3,)), dma((2,)), dma((N_FC1,)), dma((N_FC2,)),
-                dma((3, 2)), dma((3, 2)), dma((4, 2)), dma((4, 2)), dma((2,)), dma((2,)), dma((3, 2)), dma((3, 2)),
-                dma((N_FC2,)), dma((N_FC2,)), dma((2, N_FC2, 3)),
+                dma((3, 2)), dma((3, 2)), dma((4, 2)), dma((4, 2)), dma, dma, dma((4, 2)), dma((4, 2)),
+                dma((N_FC2,)), dma((N_FC2,)),
             ],
             compiler_params=pltpu.CompilerParams(
                 collective_id=0, has_side_effects=True, vmem_limit_bytes=60 * 1024 * 1024),

time: 28.6 us -> 26.7 us (0.934)
  local copies, waits for them, and re-layouts: 1.78 us -> 0.75 us
  Pallas kernels: 26.7 us -> 25.8 us
    unnamed x1, local copies, waits for them, and re-layouts: 1.78 us -> 0.75 us
    pallas_call x1, Pallas kernels: 26.7 us -> 25.8 us  [device_step(): pl.pallas_call(layer_kernel, out_shape=pltpu.VMEM((IMAGES, BLOCK, D), BF1...]
where the time goes in v4:
time: 26.7 us; the launch traced here: 26.6 us
  Pallas kernels  25.8 us (97%)
  local copies, waits for them, and re-layouts  0.75 us (3%)
    pallas_call x1, Pallas kernels, device_step(): pl.pallas_call(layer_kernel, out_shape=pltpu.VMEM((IMAGES, BLOCK, D), BF1...  25.8 us
    unnamed x1, local copies, waits for them, and re-layouts  0.75 us

profile of v4, /device:TPU:0, one launch (start us, length us, event | category | flops | bytes accessed | tf_op | source)
XLA Modules:
  0.0 26.6 jit_solution(4645535719691567766)
XLA Ops:
  0.0 25.8 %shard_map.154 = bf16[6,32,1024]{2,1,0:T(8,128)(2,1)S(1)} custom-call(f32[6,3,32,256]{3,2,1,0:T(8,128)} %bitcast.19, bf16[768,1024]{1,0:T(8,128)(2,1)} %bitcast.18, f32[8,128]{1,0:T(8,128)} %bitcast.21, bf16[32,1024]{1,0:T(8,128)(2,1)} %pos_hbm.1, f32[8,128]{1,0:T(8,128)} %bitcast.22, f32[8,128]{1,0:T(8,128)} %bitcast.23, bf16[3072,1024]{1,0:T(8,128)(2,1)} %bitcast.16, ...), custom_call_target="tpu_custom_call" | custom-call | tf_op jit(solution)/shard_map/pallas_call | solution.py:318
  25.8 0.7 %copy.18 = bf16[6,32,1024]{2,1,0:T(8,128)(2,1)} copy(bf16[6,32,1024]{2,1,0:T(8,128)(2,1)S(1)} %shard_map.154) | data formatting | bytes 786432

commit v5 on v4

--- a/solution.py
+++ b/solution.py
@@ -137,10 +137,12 @@
         copy.start()
         sends.append(copy)
 
-    def send_slot(slot):
-        for k in (2, 1, 3):
+    def send_slot(slot, where):
+        for k in where:
             to = chip_at(k)
             start(remote(xs.at[x_block(to, slot), :], xg.at[block(slot, k, 0), :], xsend.at[k - 1, slot], xrecv.at[k - 1, slot], to * 2 + core))
+
+    def share_own(slot):
         start(remote(xs.at[x_block(chip, slot), :], xg.at[block(slot, 0, 1), :], fsend.at[0, slot], frecv.at[0, slot], mate))
         xg[block(slot, 0, 0), :] = xs[x_block(chip, slot), :]
 
@@ -154,9 +156,13 @@
     bp_row = as_row(vecs[0])
     project(*part)
     pl.semaphore_wait(barrier, 7)
-    send_slot(1)
+    send_slot(1, (2, 1))
+    share_own(1)
     project(*embed(1))
-    send_slot(0)
+    send_slot(0, (2, 1))
+    send_slot(1, (3,))
+    send_slot(0, (3,))
+    share_own(0)
 
     g1_row, c1_row = as_row(vecs[1]), as_row(vecs[2])
 
@@ -177,19 +183,9 @@
     for slot in (1, 0):
         forwarded(slot, 0)
     norm_blocks([block(1, 0, 1), block(0, 0, 1)])
-    for slot in (1, 0):
-        for k in (2, 1):
-            arrive(slot, k)
-        norm_blocks([block(slot, k, 0) for k in (2, 1)])
     for c in wq_copies:
         c.wait()
     brow = [as_row(bqkv[t]) for t in range(3)]
-    for slot in (1, 0):
-        for k in (2, 1):
-            forwarded(slot, k)
-    norm_blocks([block(slot, k, 1) for slot in (1, 0) for k in (2, 1)])
-
-    early_q, early_kv = ((0, 192), (384, 512)), ((0, 192), (320, 512))
 
     def heads_of(t, dst, pieces):
         rows = jnp.concatenate([y1[a:b, :] for a, b in pieces], axis=0)
@@ -199,11 +195,26 @@
             dst[a:b, :] = got[at:at + b - a]
             at += b - a
 
-    heads_of(0, qh, early_q)
-    heads_of(1, kh, early_kv)
+    own = ((0, 64), (384, 416), (448, 480))
+    heads_of(0, qh, own)
+    heads_of(1, kh, own)
+    heads_of(2, vh, own)
+
+    for slot in (1, 0):
+        for k in (2, 1):
+            arrive(slot, k)
+        norm_blocks([block(slot, k, 0) for k in (2, 1)])
+    for slot in (1, 0):
+        for k in (2, 1):
+            forwarded(slot, k)
+    norm_blocks([block(slot, k, 1) for slot in (1, 0) for k in (2, 1)])
+    near_q = ((64, 192), (416, 448), (480, 512))
+    near_kv = ((64, 192), (320, 384), (416, 448), (480, 512))
+    heads_of(0, qh, near_q)
+    heads_of(1, kh, near_kv)
     for slot in (1, 0):
         arrive(slot, 3)
-    heads_of(2, vh, early_kv)
+    heads_of(2, vh, near_kv)
     norm_blocks([block(slot, 3, 0) for slot in (1, 0)])
     for slot in (1, 0):
         forwarded(slot, 3)

time: 26.7 us -> 26.5 us (level)
  no operation moved by 1% of the time
where the time goes in v5:
time: 26.5 us; the launch traced here: 26.3 us
  Pallas kernels  25.6 us (97%)
  local copies, waits for them, and re-layouts  0.75 us (3%)
    pallas_call x1, Pallas kernels, device_step(): pl.pallas_call(layer_kernel, out_shape=pltpu.VMEM((IMAGES, BLOCK, D), BF1...  25.6 us
    unnamed x1, local copies, waits for them, and re-layouts  0.75 us

profile of v5, /device:TPU:0, one launch (start us, length us, event | category | flops | bytes accessed | tf_op | source)
XLA Modules:
  0.0 26.3 jit_solution(12149858300835140958)
XLA Ops:
  0.0 25.6 %shard_map.154 = bf16[6,32,1024]{2,1,0:T(8,128)(2,1)S(1)} custom-call(f32[6,3,32,256]{3,2,1,0:T(8,128)} %bitcast.19, bf16[768,1024]{1,0:T(8,128)(2,1)} %bitcast.18, f32[8,128]{1,0:T(8,128)} %bitcast.21, bf16[32,1024]{1,0:T(8,128)(2,1)} %pos_hbm.1, f32[8,128]{1,0:T(8,128)} %bitcast.22, f32[8,128]{1,0:T(8,128)} %bitcast.23, bf16[3072,1024]{1,0:T(8,128)(2,1)} %bitcast.16, ...), custom_call_target="tpu_custom_call" | custom-call | tf_op jit(solution)/shard_map/pallas_call | solution.py:329
  25.6 0.7 %copy.18 = bf16[6,32,1024]{2,1,0:T(8,128)(2,1)} copy(bf16[6,32,1024]{2,1,0:T(8,128)(2,1)S(1)} %shard_map.154) | data formatting | bytes 786432

commit v6 on v4

--- a/solution.py
+++ b/solution.py
@@ -177,40 +177,12 @@
     for slot in (1, 0):
         forwarded(slot, 0)
     norm_blocks([block(1, 0, 1), block(0, 0, 1)])
-    for slot in (1, 0):
-        for k in (2, 1):
-            arrive(slot, k)
-        norm_blocks([block(slot, k, 0) for k in (2, 1)])
     for c in wq_copies:
         c.wait()
     brow = [as_row(bqkv[t]) for t in range(3)]
-    for slot in (1, 0):
-        for k in (2, 1):
-            forwarded(slot, k)
-    norm_blocks([block(slot, k, 1) for slot in (1, 0) for k in (2, 1)])
-
-    early_q, early_kv = ((0, 192), (384, 512)), ((0, 192), (320, 512))
-
-    def heads_of(t, dst, pieces):
-        rows = jnp.concatenate([y1[a:b, :] for a, b in pieces], axis=0)
-        got = (lax.dot_general(rows, wqkv[t], NT, preferred_element_type=F32) + brow[t]).astype(BF16)
-        at = 0
-        for a, b in pieces:
-            dst[a:b, :] = got[at:at + b - a]
-            at += b - a
-
-    heads_of(0, qh, early_q)
-    heads_of(1, kh, early_kv)
-    for slot in (1, 0):
-        arrive(slot, 3)
-    heads_of(2, vh, early_kv)
-    norm_blocks([block(slot, 3, 0) for slot in (1, 0)])
-    for slot in (1, 0):
-        forwarded(slot, 3)
-    norm_blocks([block(slot, 3, 1) for slot in (1, 0)])
-    heads_of(0, qh, ((192, 256),))
-    heads_of(1, kh, ((192, 320),))
-    heads_of(2, vh, ((192, 320),))
+
+    def heads_of(t, dst, a, b):
+        dst[a:b, :] = (lax.dot_general(y1[a:b, :], wqkv[t], NT, preferred_element_type=F32) + brow[t]).astype(BF16)
 
     def attend(q0, rows, k0):
         low = lax.broadcasted_iota(jnp.int32, (rows, 128), 1) < 64
@@ -228,19 +200,48 @@
                 heads.append(jnp.dot(w, v_pair, preferred_element_type=F32))
             og[q0:q0 + rows, cols] = jnp.where(low, heads[0], heads[1]).astype(BF16)
 
+    o_mate = remote(og.at[pl.ds(448, 64), :], op, osend, orecv, mate)
+
+    for k in (2, 1):
+        arrive(1, k)
+    norm_blocks([block(1, k, 0) for k in (2, 1)])
+    for k in (2, 1):
+        forwarded(1, k)
+    norm_blocks([block(1, k, 1) for k in (2, 1)])
+    arrive(1, 3)
+    norm_blocks([block(1, 3, 0)])
+    for k in (2, 1):
+        arrive(0, k)
+    norm_blocks([block(0, k, 0) for k in (2, 1)])
+    forwarded(1, 3)
+    norm_blocks([block(1, 3, 1)])
+    heads_of(0, qh, 384, 512)
+    heads_of(1, kh, 256, 512)
+    heads_of(2, vh, 256, 512)
+    for k in (2, 1):
+        forwarded(0, k)
+    norm_blocks([block(0, k, 1) for k in (2, 1)])
+    attend(384, 128, 256)
+    start(o_mate)
+
+    arrive(0, 3)
+    for t, dst in ((0, qh), (1, kh), (2, vh)):
+        heads_of(t, dst, 0, 192)
+    norm_blocks([block(0, 3, 0)])
+    forwarded(0, 3)
+    norm_blocks([block(0, 3, 1)])
+    for t, dst in ((0, qh), (1, kh), (2, vh)):
+        heads_of(t, dst, 192, 256)
+
     def o_home(k, other):
         dev = chip_at(k) * 2 + (core if other == 0 else 1 - core)
         return remote(og.at[block(0, k, other), :], oh.at[other, pl.ds(k * BLOCK, BLOCK), :],
                       hsend.at[k, other], hrecv.at[k, other], dev)
 
-    o_mate = remote(og.at[pl.ds(448, 64), :], op, osend, orecv, mate)
-
     attend(128, 128, 0)
     for k in (3, 2):
         for other in range(2):
             start(o_home(k, other))
-    attend(384, 128, 256)
-    start(o_mate)
     attend(0, 128, 0)
     for k, other in ((1, 0), (1, 1), (0, 1)):
         start(o_home(k, other))

time: 26.7 us -> 26.8 us (level)
  no operation moved by 1% of the time
where the time goes in v6:
time: 26.8 us; the launch traced here: 26.7 us
  Pallas kernels  25.9 us (97%)
  local copies, waits for them, and re-layouts  0.75 us (3%)
    pallas_call x1, Pallas kernels, device_step(): pl.pallas_call(layer_kernel, out_shape=pltpu.VMEM((IMAGES, BLOCK, D), BF1...  25.9 us
    unnamed x1, local copies, waits for them, and re-layouts  0.75 us

profile of v6, /device:TPU:0, one launch (start us, length us, event | category | flops | bytes accessed | tf_op | source)
XLA Modules:
  0.0 26.7 jit_solution(5438312310884463938)
XLA Ops:
  0.0 25.9 %shard_map.154 = bf16[6,32,1024]{2,1,0:T(8,128)(2,1)S(1)} custom-call(f32[6,3,32,256]{3,2,1,0:T(8,128)} %bitcast.19, bf16[768,1024]{1,0:T(8,128)(2,1)} %bitcast.18, f32[8,128]{1,0:T(8,128)} %bitcast.21, bf16[32,1024]{1,0:T(8,128)(2,1)} %pos_hbm.1, f32[8,128]{1,0:T(8,128)} %bitcast.22, f32[8,128]{1,0:T(8,128)} %bitcast.23, bf16[3072,1024]{1,0:T(8,128)(2,1)} %bitcast.16, ...), custom_call_target="tpu_custom_call" | custom-call | tf_op jit(solution)/shard_map/pallas_call | solution.py:319
  25.9 0.7 %copy.18 = bf16[6,32,1024]{2,1,0:T(8,128)(2,1)} copy(bf16[6,32,1024]{2,1,0:T(8,128)(2,1)S(1)} %shard_map.154) | data formatting | bytes 786432

commit v7 on v6

--- a/solution.py
+++ b/solution.py
@@ -145,18 +145,20 @@
         xg[block(slot, 0, 0), :] = xs[x_block(chip, slot), :]
 
     small_copies[0].wait()
+    for c in wq_copies:
+        c.start()
     part = embed(0)
     for c in small_copies[2:]:
         c.wait()
     small_copies[1].wait()
-    for c in wq_copies + wo_copies + w1_copies + w2_copies:
-        c.start()
     bp_row = as_row(vecs[0])
     project(*part)
     pl.semaphore_wait(barrier, 7)
     send_slot(1)
     project(*embed(1))
     send_slot(0)
+    for c in wo_copies + w1_copies + w2_copies:
+        c.start()
 
     g1_row, c1_row = as_row(vecs[1]), as_row(vecs[2])
 
@@ -177,8 +179,6 @@
     for slot in (1, 0):
         forwarded(slot, 0)
     norm_blocks([block(1, 0, 1), block(0, 0, 1)])
-    for c in wq_copies:
-        c.wait()
     brow = [as_row(bqkv[t]) for t in range(3)]
 
     def heads_of(t, dst, a, b):
@@ -215,6 +215,8 @@
     norm_blocks([block(0, k, 0) for k in (2, 1)])
     forwarded(1, 3)
     norm_blocks([block(1, 3, 1)])
+    for c in wq_copies:
+        c.wait()
     heads_of(0, qh, 384, 512)
     heads_of(1, kh, 256, 512)
     heads_of(2, vh, 256, 512)

time: 26.8 us -> 27 us (level)
  no operation moved by 1% of the time
where the time goes in v7:
time: 27 us; the launch traced here: 26.9 us
  Pallas kernels  26.1 us (97%)
  local copies, waits for them, and re-layouts  0.75 us (3%)
    pallas_call x1, Pallas kernels, device_step(): pl.pallas_call(layer_kernel, out_shape=pltpu.VMEM((IMAGES, BLOCK, D), BF1...  26.1 us
    unnamed x1, local copies, waits for them, and re-layouts  0.75 us

profile of v7, /device:TPU:0, one launch (start us, length us, event | category | flops | bytes accessed | tf_op | source)
XLA Modules:
  0.0 26.9 jit_solution(9284854299991510711)
XLA Ops:
  0.0 26.1 %shard_map.154 = bf16[6,32,1024]{2,1,0:T(8,128)(2,1)S(1)} custom-call(f32[6,3,32,256]{3,2,1,0:T(8,128)} %bitcast.19, bf16[768,1024]{1,0:T(8,128)(2,1)} %bitcast.18, f32[8,128]{1,0:T(8,128)} %bitcast.21, bf16[32,1024]{1,0:T(8,128)(2,1)} %pos_hbm.1, f32[8,128]{1,0:T(8,128)} %bitcast.22, f32[8,128]{1,0:T(8,128)} %bitcast.23, bf16[3072,1024]{1,0:T(8,128)(2,1)} %bitcast.16, ...), custom_call_target="tpu_custom_call" | custom-call | tf_op jit(solution)/shard_map/pallas_call | solution.py:321
  26.1 0.7 %copy.18 = bf16[6,32,1024]{2,1,0:T(8,128)(2,1)} copy(bf16[6,32,1024]{2,1,0:T(8,128)(2,1)S(1)} %shard_map.154) | data formatting | bytes 786432

commit v8 on v5

--- a/solution.py
+++ b/solution.py
@@ -225,18 +225,19 @@
 
     def attend(q0, rows, k0):
         low = lax.broadcasted_iota(jnp.int32, (rows, 128), 1) < 64
-        for pair in range(4):
-            cols = slice(pair * 128, (pair + 1) * 128)
+        pairs = [slice(pair * 128, (pair + 1) * 128) for pair in range(4)]
+        scores = []
+        for cols in pairs:
             q_pair = qh[q0:q0 + rows, cols]
-            k_pair = kh[k0:k0 + 256, cols]
-            v_pair = vh[k0:k0 + 256, cols]
-            heads = []
             for h in range(2):
                 q_one = jnp.where(low == (h == 0), q_pair, jnp.zeros_like(q_pair))
-                s = lax.dot_general(q_one, k_pair, NT, preferred_element_type=F32)
-                e = jnp.exp2((s - jnp.max(s, axis=-1, keepdims=True)) * EXP_SCALE)
-                w = (e * (1.0 / jnp.sum(e, axis=-1, keepdims=True))).astype(BF16)
-                heads.append(jnp.dot(w, v_pair, preferred_element_type=F32))
+                scores.append(lax.dot_general(q_one, kh[k0:k0 + 256, cols], NT, preferred_element_type=F32))
+        weights = []
+        for s in scores:
+            e = jnp.exp2((s - jnp.max(s, axis=-1, keepdims=True)) * EXP_SCALE)
+            weights.append((e * (1.0 / jnp.sum(e, axis=-1, keepdims=True))).astype(BF16))
+        for i, cols in enumerate(pairs):
+            heads = [jnp.dot(weights[2 * i + h], vh[k0:k0 + 256, cols], preferred_element_type=F32) for h in range(2)]
             og[q0:q0 + rows, cols] = jnp.where(low, heads[0], heads[1]).astype(BF16)
 
     def o_home(k, other):

time: 26.5 us -> 25.8 us (0.974)
  Pallas kernels: 25.6 us -> 24.9 us
    pallas_call x1, Pallas kernels: 25.6 us -> 24.9 us  [device_step(): pl.pallas_call(layer_kernel, out_shape=pltpu.VMEM((IMAGES, BLOCK, D), BF1...]
where the time goes in v8:
time: 25.8 us; the launch traced here: 25.7 us
  Pallas kernels  24.9 us (97%)
  local copies, waits for them, and re-layouts  0.75 us (3%)
    pallas_call x1, Pallas kernels, device_step(): pl.pallas_call(layer_kernel, out_shape=pltpu.VMEM((IMAGES, BLOCK, D), BF1...  24.9 us
    unnamed x1, local copies, waits for them, and re-layouts  0.75 us

profile of v8, /device:TPU:0, one launch (start us, length us, event | category | flops | bytes accessed | tf_op | source)
XLA Modules:
  0.0 25.7 jit_solution(6063483833535928515)
XLA Ops:
  0.0 24.9 %shard_map.154 = bf16[6,32,1024]{2,1,0:T(8,128)(2,1)S(1)} custom-call(f32[6,3,32,256]{3,2,1,0:T(8,128)} %bitcast.19, bf16[768,1024]{1,0:T(8,128)(2,1)} %bitcast.18, f32[8,128]{1,0:T(8,128)} %bitcast.21, bf16[32,1024]{1,0:T(8,128)(2,1)} %pos_hbm.1, f32[8,128]{1,0:T(8,128)} %bitcast.22, f32[8,128]{1,0:T(8,128)} %bitcast.23, bf16[3072,1024]{1,0:T(8,128)(2,1)} %bitcast.16, ...), custom_call_target="tpu_custom_call" | custom-call | tf_op jit(solution)/shard_map/pallas_call | solution.py:330
  24.9 0.7 %copy.18 = bf16[6,32,1024]{2,1,0:T(8,128)(2,1)} copy(bf16[6,32,1024]{2,1,0:T(8,128)(2,1)S(1)} %shard_map.154) | data formatting | bytes 786432

commit v9 on v5

--- a/solution.py
+++ b/solution.py
@@ -195,6 +195,32 @@
             dst[a:b, :] = got[at:at + b - a]
             at += b - a
 
+    pairs = [slice(pair * 128, (pair + 1) * 128) for pair in range(4)]
+    low = lax.broadcasted_iota(jnp.int32, (128, 128), 1) < 64
+
+    def score(q0, k0):
+        scores = []
+        for cols in pairs:
+            q_pair = qh[q0:q0 + 128, cols]
+            for h in range(2):
+                q_one = jnp.where(low == (h == 0), q_pair, jnp.zeros_like(q_pair))
+                scores.append(lax.dot_general(q_one, kh[k0:k0 + 256, cols], NT, preferred_element_type=F32))
+        return scores
+
+    def soften(scores):
+        weights = []
+        for s in scores:
+            e = jnp.exp2((s - jnp.max(s, axis=-1, keepdims=True)) * EXP_SCALE)
+            weights.append((e * (1.0 / jnp.sum(e, axis=-1, keepdims=True))).astype(BF16))
+        return weights
+
+    def combine(weights, q0, k0):
+        for i, cols in enumerate(pairs):
+            heads = [jnp.dot(weights[2 * i + h], vh[k0:k0 + 256, cols], preferred_element_type=F32) for h in range(2)]
+            og[q0:q0 + 128, cols] = jnp.where(low, heads[0], heads[1]).astype(BF16)
+
+    o_mate = remote(og.at[pl.ds(448, 64), :], op, osend, orecv, mate)
+
     own = ((0, 64), (384, 416), (448, 480))
     heads_of(0, qh, own)
     heads_of(1, kh, own)
@@ -212,47 +238,34 @@
     near_kv = ((64, 192), (320, 384), (416, 448), (480, 512))
     heads_of(0, qh, near_q)
     heads_of(1, kh, near_kv)
-    for slot in (1, 0):
-        arrive(slot, 3)
+    arrive(1, 3)
     heads_of(2, vh, near_kv)
-    norm_blocks([block(slot, 3, 0) for slot in (1, 0)])
-    for slot in (1, 0):
-        forwarded(slot, 3)
-    norm_blocks([block(slot, 3, 1) for slot in (1, 0)])
-    heads_of(0, qh, ((192, 256),))
-    heads_of(1, kh, ((192, 320),))
-    heads_of(2, vh, ((192, 320),))
-
-    def attend(q0, rows, k0):
-        low = lax.broadcasted_iota(jnp.int32, (rows, 128), 1) < 64
-        for pair in range(4):
-            cols = slice(pair * 128, (pair + 1) * 128)
-            q_pair = qh[q0:q0 + rows, cols]
-            k_pair = kh[k0:k0 + 256, cols]
-            v_pair = vh[k0:k0 + 256, cols]
-            heads = []
-            for h in range(2):
-                q_one = jnp.where(low == (h == 0), q_pair, jnp.zeros_like(q_pair))
-                s = lax.dot_general(q_one, k_pair, NT, preferred_element_type=F32)
-                e = jnp.exp2((s - jnp.max(s, axis=-1, keepdims=True)) * EXP_SCALE)
-                w = (e * (1.0 / jnp.sum(e, axis=-1, keepdims=True))).astype(BF16)
-                heads.append(jnp.dot(w, v_pair, preferred_element_type=F32))
-            og[q0:q0 + rows, cols] = jnp.where(low, heads[0], heads[1]).astype(BF16)
+    norm_blocks([block(1, 3, 0)])
+    forwarded(1, 3)
+    norm_blocks([block(1, 3, 1)])
+    heads_of(1, kh, ((256, 320),))
+    heads_of(2, vh, ((256, 320),))
+    arrive(0, 3)
+    combine(soften(score(384, 256)), 384, 256)
+    start(o_mate)
+    norm_blocks([block(0, 3, 0)])
+    forwarded(0, 3)
+    norm_blocks([block(0, 3, 1)])
+    for t, dst in ((0, qh), (1, kh), (2, vh)):
+        heads_of(t, dst, ((192, 256),))
 
     def o_home(k, other):
         dev = chip_at(k) * 2 + (core if other == 0 else 1 - core)
         return remote(og.at[block(0, k, other), :], oh.at[other, pl.ds(k * BLOCK, BLOCK), :],
                       hsend.at[k, other], hrecv.at[k, other], dev)
 
-    o_mate = remote(og.at[pl.ds(448, 64), :], op, osend, orecv, mate)
-
-    attend(128, 128, 0)
+    late = soften(score(128, 0))
+    scores = score(0, 0)
+    combine(late, 128, 0)
     for k in (3, 2):
         for other in range(2):
             start(o_home(k, other))
-    attend(384, 128, 256)
-    start(o_mate)
-    attend(0, 128, 0)
+    combine(soften(scores), 0, 0)
     for k, other in ((1, 0), (1, 1), (0, 1)):
         start(o_home(k, other))
 

time: 26.5 us -> 27.7 us (1.045)
  Pallas kernels: 25.6 us -> 26.8 us
    pallas_call x1, Pallas kernels: 25.6 us -> 26.8 us  [device_step(): pl.pallas_call(layer_kernel, out_shape=pltpu.VMEM((IMAGES, BLOCK, D), BF1...]
where the time goes in v9:
time: 27.7 us; the launch traced here: 27.6 us
  Pallas kernels  26.8 us (97%)
  local copies, waits for them, and re-layouts  0.75 us (3%)
    pallas_call x1, Pallas kernels, device_step(): pl.pallas_call(layer_kernel, out_shape=pltpu.VMEM((IMAGES, BLOCK, D), BF1...  26.8 us
    unnamed x1, local copies, waits for them, and re-layouts  0.75 us

profile of v9, /device:TPU:0, one launch (start us, length us, event | category | flops | bytes accessed | tf_op | source)
XLA Modules:
  0.0 27.6 jit_solution(13397770229872111475)
XLA Ops:
  0.0 26.8 %shard_map.154 = bf16[6,32,1024]{2,1,0:T(8,128)(2,1)S(1)} custom-call(f32[6,3,32,256]{3,2,1,0:T(8,128)} %bitcast.19, bf16[768,1024]{1,0:T(8,128)(2,1)} %bitcast.18, f32[8,128]{1,0:T(8,128)} %bitcast.21, bf16[32,1024]{1,0:T(8,128)(2,1)} %pos_hbm.1, f32[8,128]{1,0:T(8,128)} %bitcast.22, f32[8,128]{1,0:T(8,128)} %bitcast.23, bf16[3072,1024]{1,0:T(8,128)(2,1)} %bitcast.16, ...), custom_call_target="tpu_custom_call" | custom-call | tf_op jit(solution)/shard_map/pallas_call | solution.py:342
  26.9 0.7 %copy.18 = bf16[6,32,1024]{2,1,0:T(8,128)(2,1)} copy(bf16[6,32,1024]{2,1,0:T(8,128)(2,1)S(1)} %shard_map.154) | data formatting | bytes 786432

commit v10 on v8

--- a/solution.py
+++ b/solution.py
@@ -16,7 +16,7 @@
 BLOCK = 32
 TOKENS = 256
 OWN = 192
-HALF = 128
+HALF = 96
 N_FC1, W_FC1 = 8, 512
 N_FC2, W_FC2 = 2, 512
 EXP_SCALE = math.log2(math.e) / 8.0
@@ -242,17 +242,18 @@
 
     def o_home(k, other):
         dev = chip_at(k) * 2 + (core if other == 0 else 1 - core)
-        return remote(og.at[block(0, k, other), :], oh.at[other, pl.ds(k * BLOCK, BLOCK), :],
+        return remote(og.at[block(0, k, other), :], oh.at[other, pl.ds((k + 1) // 2 * BLOCK, BLOCK), :],
                       hsend.at[k, other], hrecv.at[k, other], dev)
 
-    o_mate = remote(og.at[pl.ds(448, 64), :], op, osend, orecv, mate)
+    o_mates = [remote(og.at[src, :], op.at[dst, :], osend.at[i], orecv.at[i], mate)
+               for i, (src, dst) in enumerate(((block(0, 2, 1), pl.ds(0, 32)), (pl.ds(448, 64), pl.ds(32, 64))))]
 
     attend(128, 128, 0)
-    for k in (3, 2):
-        for other in range(2):
-            start(o_home(k, other))
+    for other in range(2):
+        start(o_home(3, other))
+    start(o_mates[0])
     attend(384, 128, 256)
-    start(o_mate)
+    start(o_mates[1])
     attend(0, 128, 0)
     for k, other in ((1, 0), (1, 1), (0, 1)):
         start(o_home(k, other))
@@ -284,33 +285,42 @@
         cols = slice(j * W_FC2, (j + 1) * W_FC2)
         return (jnp.dot(hid[0:m, :], w2[j], preferred_element_type=F32) + (res[0:m, cols] + b2_row[:, cols])).astype(BF16)
 
-    def shared_home(j, recv):
+    def back_home(i, j, recv):
         other = chip_at(2)
-        image = 4 + (other if recv else chip) // 2
-        return remote(back.at[j], out.at[image, :, pl.ds(j * W_FC2, W_FC2)], rsend.at[j], rrecv.at[j], other * 2 + core)
-
-    finish(64, xg[384:448, :], og[384:448, :], op, o_mate.wait_recv)
+        image = other if recv else chip
+        if i == 1:
+            image = 4 + image // 2
+        return remote(back.at[i, j], out.at[image, :, pl.ds(j * W_FC2, W_FC2)], rsend.at[i, j], rrecv.at[i, j], other * 2 + core)
+
+    def mate_ready():
+        for c in o_mates:
+            c.wait_recv()
+
+    finish(96, jnp.concatenate([xg[128:160, :], xg[384:448, :]], axis=0), jnp.concatenate([og[128:160, :], og[384:448, :]], axis=0),
+           op, mate_ready)
     for j in range(N_FC2):
-        rows = second(64, j)
-        back[j] = rows[BLOCK:]
-        start(shared_home(j, False))
-        out[4 + cy, :, j * W_FC2:(j + 1) * W_FC2] = rows[0:BLOCK]
+        rows = second(96, j)
+        for i in range(2):
+            back[i, j] = rows[64 * i:64 * i + BLOCK]
+            start(back_home(i, j, False))
+        out[4 + cy, :, j * W_FC2:(j + 1) * W_FC2] = rows[BLOCK:2 * BLOCK]
 
     def home_ready():
-        for k in range(4):
+        for k in (0, 1, 3):
             o_home(k, 1).wait_recv()
 
-    for k in (1, 2, 3):
+    for k in (1, 3):
         o_home(k, 0).wait_recv()
-    finish(128, jnp.concatenate([xg[0:32, :]] + [xs[x_block(chip_at(k), 0), :] for k in (1, 2, 3)], axis=0),
-           jnp.concatenate([og[0:32, :], oh[0, 32:128, :]], axis=0), oh.at[1], home_ready)
+    finish(96, jnp.concatenate([xg[0:32, :]] + [xs[x_block(chip_at(k), 0), :] for k in (1, 3)], axis=0),
+           jnp.concatenate([og[0:32, :], oh[0, 32:96, :]], axis=0), oh.at[1], home_ready)
     for j in range(N_FC2):
-        rows = second(128, j)
-        for k in range(4):
-            out[chip_at(k), :, j * W_FC2:(j + 1) * W_FC2] = rows[k * BLOCK:(k + 1) * BLOCK]
+        rows = second(96, j)
+        for i, k in enumerate((0, 1, 3)):
+            out[chip_at(k), :, j * W_FC2:(j + 1) * W_FC2] = rows[i * BLOCK:(i + 1) * BLOCK]
 
     for j in range(N_FC2):
-        shared_home(j, True).wait_recv()
+        for i in range(2):
+            back_home(i, j, True).wait_recv()
     for c in sends:
         c.wait_send()
 
@@ -339,12 +349,12 @@
                 vm((3 * OWN, 2048), BF16), vm((2048, 256), BF16), vm((OWN, 768), BF16), vm((OWN, D), BF16),
                 vm((2 * TOKENS, D), BF16), vm((2 * TOKENS, D), BF16),
                 vm((512, 512), BF16), vm((512, 512), BF16), vm((512, 512), BF16), vm((512, 512), BF16),
-                vm((64, 512), BF16), vm((2, HALF, 512), BF16),
-                vm((HALF, D), F32), vm((HALF, D), BF16), vm((HALF, FF), BF16), vm((N_FC2, BLOCK, W_FC2), BF16),
+                vm((HALF, 512), BF16), vm((2, HALF, 512), BF16),
+                vm((HALF, D), F32), vm((HALF, D), BF16), vm((HALF, FF), BF16), vm((2, N_FC2, BLOCK, W_FC2), BF16),
                 vm((N_FC1, 1, W_FC1), F32), vm((2, HALF, W_FC1), F32),
                 dma((13,)), dma((3,)), dma((2,)), dma((N_FC1,)), dma((N_FC2,)),
-                dma((3, 2)), dma((3, 2)), dma((4, 2)), dma((4, 2)), dma, dma, dma((4, 2)), dma((4, 2)),
-                dma((N_FC2,)), dma((N_FC2,)),
+                dma((3, 2)), dma((3, 2)), dma((4, 2)), dma((4, 2)), dma((2,)), dma((2,)), dma((4, 2)), dma((4, 2)),
+                dma((2, N_FC2)), dma((2, N_FC2)),
             ],
             compiler_params=pltpu.CompilerParams(
                 collective_id=0, has_side_effects=True, vmem_limit_bytes=60 * 1024 * 1024),

time: 25.8 us -> 26.4 us (1.023)
  Pallas kernels: 24.9 us -> 25.5 us
    pallas_call x1, Pallas kernels: 24.9 us -> 25.5 us  [device_step(): pl.pallas_call(layer_kernel, out_shape=pltpu.VMEM((IMAGES, BLOCK, D), BF1...]
where the time goes in v10:
time: 26.4 us; the launch traced here: 26.3 us
  Pallas kernels  25.5 us (97%)
  local copies, waits for them, and re-layouts  0.75 us (3%)
    pallas_call x1, Pallas kernels, device_step(): pl.pallas_call(layer_kernel, out_shape=pltpu.VMEM((IMAGES, BLOCK, D), BF1...  25.5 us
    unnamed x1, local copies, waits for them, and re-layouts  0.75 us

profile of v10, /device:TPU:0, one launch (start us, length us, event | category | flops | bytes accessed | tf_op | source)
XLA Modules:
  0.0 26.3 jit_solution(479723810683695769)
XLA Ops:
  0.0 25.5 %shard_map.154 = bf16[6,32,1024]{2,1,0:T(8,128)(2,1)S(1)} custom-call(f32[6,3,32,256]{3,2,1,0:T(8,128)} %bitcast.19, bf16[768,1024]{1,0:T(8,128)(2,1)} %bitcast.18, f32[8,128]{1,0:T(8,128)} %bitcast.21, bf16[32,1024]{1,0:T(8,128)(2,1)} %pos_hbm.1, f32[8,128]{1,0:T(8,128)} %bitcast.22, f32[8,128]{1,0:T(8,128)} %bitcast.23, bf16[3072,1024]{1,0:T(8,128)(2,1)} %bitcast.16, ...), custom_call_target="tpu_custom_call" | custom-call | tf_op jit(solution)/shard_map/pallas_call | solution.py:340
  25.5 0.7 %copy.18 = bf16[6,32,1024]{2,1,0:T(8,128)(2,1)} copy(bf16[6,32,1024]{2,1,0:T(8,128)(2,1)S(1)} %shard_map.154) | data formatting | bytes 786432

commit v11 on v8

--- a/solution.py
+++ b/solution.py
@@ -223,22 +223,29 @@
     heads_of(1, kh, ((192, 320),))
     heads_of(2, vh, ((192, 320),))
 
-    def attend(q0, rows, k0):
-        low = lax.broadcasted_iota(jnp.int32, (rows, 128), 1) < 64
-        pairs = [slice(pair * 128, (pair + 1) * 128) for pair in range(4)]
+    pairs = [slice(pair * 128, (pair + 1) * 128) for pair in range(4)]
+    low = lax.broadcasted_iota(jnp.int32, (128, 128), 1) < 64
+
+    def score(q0, k0):
         scores = []
         for cols in pairs:
-            q_pair = qh[q0:q0 + rows, cols]
+            q_pair = qh[q0:q0 + 128, cols]
             for h in range(2):
                 q_one = jnp.where(low == (h == 0), q_pair, jnp.zeros_like(q_pair))
                 scores.append(lax.dot_general(q_one, kh[k0:k0 + 256, cols], NT, preferred_element_type=F32))
+        return scores
+
+    def soften(scores):
         weights = []
         for s in scores:
             e = jnp.exp2((s - jnp.max(s, axis=-1, keepdims=True)) * EXP_SCALE)
             weights.append((e * (1.0 / jnp.sum(e, axis=-1, keepdims=True))).astype(BF16))
+        return weights
+
+    def combine(weights, q0, k0):
         for i, cols in enumerate(pairs):
             heads = [jnp.dot(weights[2 * i + h], vh[k0:k0 + 256, cols], preferred_element_type=F32) for h in range(2)]
-            og[q0:q0 + rows, cols] = jnp.where(low, heads[0], heads[1]).astype(BF16)
+            og[q0:q0 + 128, cols] = jnp.where(low, heads[0], heads[1]).astype(BF16)
 
     def o_home(k, other):
         dev = chip_at(k) * 2 + (core if other == 0 else 1 - core)
@@ -247,13 +254,15 @@
 
     o_mate = remote(og.at[pl.ds(448, 64), :], op, osend, orecv, mate)
 
-    attend(128, 128, 0)
+    combine(soften(score(128, 0)), 128, 0)
     for k in (3, 2):
         for other in range(2):
             start(o_home(k, other))
-    attend(384, 128, 256)
+    shared = soften(score(384, 256))
+    scores = score(0, 0)
+    combine(shared, 384, 256)
     start(o_mate)
-    attend(0, 128, 0)
+    combine(soften(scores), 0, 0)
     for k, other in ((1, 0), (1, 1), (0, 1)):
         start(o_home(k, other))
 

time: 25.8 us -> 25.8 us (level)
  no operation moved by 1% of the time
where the time goes in v11:
time: 25.8 us; the launch traced here: 25.6 us
  Pallas kernels  24.9 us (97%)
  local copies, waits for them, and re-layouts  0.75 us (3%)
    pallas_call x1, Pallas kernels, device_step(): pl.pallas_call(layer_kernel, out_shape=pltpu.VMEM((IMAGES, BLOCK, D), BF1...  24.9 us
    unnamed x1, local copies, waits for them, and re-layouts  0.75 us

profile of v11, /device:TPU:0, one launch (start us, length us, event | category | flops | bytes accessed | tf_op | source)
XLA Modules:
  0.0 25.6 jit_solution(237718586956437480)
XLA Ops:
  0.0 24.9 %shard_map.154 = bf16[6,32,1024]{2,1,0:T(8,128)(2,1)S(1)} custom-call(f32[6,3,32,256]{3,2,1,0:T(8,128)} %bitcast.19, bf16[768,1024]{1,0:T(8,128)(2,1)} %bitcast.18, f32[8,128]{1,0:T(8,128)} %bitcast.21, bf16[32,1024]{1,0:T(8,128)(2,1)} %pos_hbm.1, f32[8,128]{1,0:T(8,128)} %bitcast.22, f32[8,128]{1,0:T(8,128)} %bitcast.23, bf16[3072,1024]{1,0:T(8,128)(2,1)} %bitcast.16, ...), custom_call_target="tpu_custom_call" | custom-call | tf_op jit(solution)/shard_map/pallas_call | solution.py:339
  24.9 0.7 %copy.18 = bf16[6,32,1024]{2,1,0:T(8,128)(2,1)} copy(bf16[6,32,1024]{2,1,0:T(8,128)(2,1)S(1)} %shard_map.154) | data formatting | bytes 786432

commit v12 on v11

--- a/solution.py
+++ b/solution.py
@@ -160,8 +160,8 @@
     share_own(1)
     project(*embed(1))
     send_slot(0, (2, 1))
+    send_slot(0, (3,))
     send_slot(1, (3,))
-    send_slot(0, (3,))
     share_own(0)
 
     g1_row, c1_row = as_row(vecs[1]), as_row(vecs[2])
@@ -212,16 +212,14 @@
     near_kv = ((64, 192), (320, 384), (416, 448), (480, 512))
     heads_of(0, qh, near_q)
     heads_of(1, kh, near_kv)
-    for slot in (1, 0):
-        arrive(slot, 3)
+    arrive(0, 3)
     heads_of(2, vh, near_kv)
-    norm_blocks([block(slot, 3, 0) for slot in (1, 0)])
-    for slot in (1, 0):
-        forwarded(slot, 3)
-    norm_blocks([block(slot, 3, 1) for slot in (1, 0)])
-    heads_of(0, qh, ((192, 256),))
-    heads_of(1, kh, ((192, 320),))
-    heads_of(2, vh, ((192, 320),))
+    norm_blocks([block(0, 3, 0)])
+    forwarded(0, 3)
+    norm_blocks([block(0, 3, 1)])
+    for t, dst in ((0, qh), (1, kh), (2, vh)):
+        heads_of(t, dst, ((192, 256),))
+    arrive(1, 3)
 
     pairs = [slice(pair * 128, (pair + 1) * 128) for pair in range(4)]
     low = lax.broadcasted_iota(jnp.int32, (128, 128), 1) < 64
@@ -258,6 +256,11 @@
     for k in (3, 2):
         for other in range(2):
             start(o_home(k, other))
+    norm_blocks([block(1, 3, 0)])
+    forwarded(1, 3)
+    norm_blocks([block(1, 3, 1)])
+    heads_of(1, kh, ((256, 320),))
+    heads_of(2, vh, ((256, 320),))
     shared = soften(score(384, 256))
     scores = score(0, 0)
     combine(shared, 384, 256)

time: 25.8 us -> 26.6 us (1.031)
  Pallas kernels: 24.9 us -> 25.8 us
    pallas_call x1, Pallas kernels: 24.9 us -> 25.8 us  [device_step(): pl.pallas_call(layer_kernel, out_shape=pltpu.VMEM((IMAGES, BLOCK, D), BF1...]
where the time goes in v12:
time: 26.6 us; the launch traced here: 26.5 us
  Pallas kernels  25.8 us (97%)
  local copies, waits for them, and re-layouts  0.75 us (3%)
    pallas_call x1, Pallas kernels, device_step(): pl.pallas_call(layer_kernel, out_shape=pltpu.VMEM((IMAGES, BLOCK, D), BF1...  25.8 us
    unnamed x1, local copies, waits for them, and re-layouts  0.75 us

profile of v12, /device:TPU:0, one launch (start us, length us, event | category | flops | bytes accessed | tf_op | source)
XLA Modules:
  0.0 26.5 jit_solution(9066869207867177148)
XLA Ops:
  0.0 25.8 %shard_map.154 = bf16[6,32,1024]{2,1,0:T(8,128)(2,1)S(1)} custom-call(f32[6,3,32,256]{3,2,1,0:T(8,128)} %bitcast.19, bf16[768,1024]{1,0:T(8,128)(2,1)} %bitcast.18, f32[8,128]{1,0:T(8,128)} %bitcast.21, bf16[32,1024]{1,0:T(8,128)(2,1)} %pos_hbm.1, f32[8,128]{1,0:T(8,128)} %bitcast.22, f32[8,128]{1,0:T(8,128)} %bitcast.23, bf16[3072,1024]{1,0:T(8,128)(2,1)} %bitcast.16, ...), custom_call_target="tpu_custom_call" | custom-call | tf_op jit(solution)/shard_map/pallas_call | solution.py:342
  25.8 0.7 %copy.18 = bf16[6,32,1024]{2,1,0:T(8,128)(2,1)} copy(bf16[6,32,1024]{2,1,0:T(8,128)(2,1)S(1)} %shard_map.154) | data formatting | bytes 786432
